TPU v7x, 32 devices: a whole 2x2x4 slice. The times are simulated.
32 devices in a mesh: ctx: 16 (over z, x, core), wt: 2 (over y).
Axes of the slice: x: 2, y: 2, z: 4, core: 2. Of those that a mesh axis runs over, the one named last changes fastest.
Arguments:
- patches: bfloat16 [8192, 1280], P('ctx'), may hold values from -6 to 6
- vit_gain: float32 [1280], replicated, may hold values from 0.5 to 1.5
- vit_codes: bfloat16 [1280, 3, 1280], P(None, None, 'wt'), may hold values from -1 to 1
- vit_scales: bfloat16 [2], P('wt'), may hold values from 0.5 to 2
- vit_bias: float32 [3, 1280], P(None, 'wt'), may hold values from -3 to 3
- window_ids: int32 [8192], P('ctx'), may hold values from 63 to 8191, as said below
- merger_codes: bfloat16 [4, 1280, 8192], P(None, 'wt', 'ctx'), may hold values from -0.078125 to 0.078125
- merger_scales: bfloat16 [1, 2, 8192], P(None, 'wt', 'ctx'), may hold values from 0.5 to 2
- merger_bias: float32 [8192], P('wt'), may hold values from -3 to 3
- positions: int32 [2048], P('ctx'), may hold values from 0 to 8191, as said below
- text_embed: bfloat16 [8192, 8192], P('ctx', 'wt'), may hold values from -6 to 6
- norm_gain: float32 [8192], P('wt'), may hold values from 0.5 to 1.5
- llm_codes: bfloat16 [8192, 8, 768], P('wt', None, 'ctx'), may hold values from -1 to 1
- llm_scales: bfloat16 [2, 8, 768], P('wt', None, 'ctx'), may hold values from 0.5 to 2
- llm_bias: float32 [8, 768], P('wt'), may hold values from -3 to 3
- segments: int32 [8192], P('ctx'), may hold values from 0 to 7, never falling along the last dimension, each value on 1 to 2048 neighbouring positions
Outputs:
- attention_out: bfloat16 [8192, 4096], P('ctx', 'wt')
Inputs may be any that keep to these rules, and one draw needn't show every extreme that they name: `window_ids`: windows are runs of consecutive patches of at most 64, never crossing a block of 512 patches; patches of one window share the id, different windows have different ids. `positions`: distinct. The 128 entries of one aligned block (one device's merged tokens) put at most 16 into any one block of 512 positions, and exactly 16 into some block. `segments`: never falling; each run of equal ids is at most 2048 positions long.
All inputs are finite; a program needn't handle non-finite values.
Results may differ from a plain program's by a relative error of at most 0.025.
Values may be sent and summed in bfloat16 or wider, within the bound.
No kernel may reach another device: no remote copies, remote signals or barrier semaphores. Data moves between devices by JAX's collectives and lax.ppermute only.
A program may use at most 192 MiB of HBM per device.

v0:
```python
import jax
import jax.numpy as jnp
from jax import lax
from jax.sharding import PartitionSpec as P

VHD = 80
D = 8192
KVH = 8
HD = 128
GROUP = 4
MERGE = 4
REACH = 4


VIT_EPS = 1e-06
RMS_EPS = 1e-06
ROPE_BASE = 1000000.0
FILL_LOW = -1e30


def passed_along(value, axis, steps):
    count = lax.axis_size(axis)
    leading, last = (max(0, -steps), min(count, count - steps))
    return lax.ppermute(value, axis, [(source, source + steps) for source in range(leading, last)])


def softmax_rows(scores, allowed):
    masked = jnp.where(allowed, scores, FILL_LOW)
    highest = jnp.max(masked, axis=-1, keepdims=True)
    raised = jnp.exp(masked - highest)
    return raised / jnp.sum(raised, axis=-1, keepdims=True)


def vision_norm_rows(patches, vit_gain):
    values = patches.astype(jnp.float32)
    mean_square = jnp.mean(values * values, axis=1, keepdims=True)
    return (values * lax.rsqrt(mean_square + VIT_EPS) * vit_gain).astype(jnp.bfloat16)


def window_attention(normed, weight_block, bias_block, window_ids):
    row_count = normed.shape[0]
    packed = jnp.dot(
        normed, weight_block.reshape(normed.shape[1], -1), preferred_element_type=jnp.float32
    )
    triple = (packed.reshape(row_count, 3, -1) + bias_block).astype(jnp.bfloat16)
    heads_here = triple.shape[2] // VHD
    queries = triple[:, 0].reshape(row_count, heads_here, VHD)
    keys_here = triple[:, 1].reshape(row_count, heads_here, VHD)
    values_here = triple[:, 2].reshape(row_count, heads_here, VHD)
    scores = jnp.einsum(
        "qhd,khd->hqk", queries, keys_here, preferred_element_type=jnp.float32
    ) * VHD ** (-0.5)
    allowed = window_ids[:, None] == window_ids[None, :]
    softmaxed = softmax_rows(scores, allowed[None]).astype(jnp.bfloat16)
    blended = jnp.einsum("hqk,khd->qhd", softmaxed, values_here, preferred_element_type=jnp.float32)
    return blended.astype(jnp.bfloat16).reshape(row_count, -1)


def rope_tables(first, length):
    places = (first + jnp.arange(length, dtype=jnp.int32)).astype(jnp.float32)
    frequency = ROPE_BASE ** (-jnp.arange(0, HD, 2).astype(jnp.float32) / HD)
    angles = places[:, None] * frequency[None, :]
    angles = jnp.concatenate([angles, angles], axis=1)
    return (jnp.cos(angles), jnp.sin(angles))


def rotary(inputs, cosine, sine):
    halfway = inputs.shape[-1] // 2
    turned = jnp.concatenate([-inputs[..., halfway:], inputs[..., :halfway]], axis=-1)
    return inputs * cosine + turned * sine


def split_heads(triple, cosine, sine):
    row_count, group_count = (triple.shape[0], triple.shape[1])
    queries = triple[:, :, : GROUP * HD].reshape(row_count, group_count, GROUP, HD)
    queries = rotary(queries, cosine[:, None, None, :], sine[:, None, None, :]).astype(jnp.bfloat16)
    keys_rot = rotary(
        triple[:, :, GROUP * HD : (GROUP + 1) * HD], cosine[:, None, :], sine[:, None, :]
    ).astype(jnp.bfloat16)
    values_cut = triple[:, :, (GROUP + 1) * HD :].astype(jnp.bfloat16)
    return (queries, keys_rot, values_cut)


def merge_project(features, merger_codes, merger_scales, merger_bias):
    row_count = features.shape[0]
    flat = features.reshape(row_count, -1)
    codes_piece = lax.all_gather(merger_codes, "ctx", axis=2, tiled=True)
    scale_piece = lax.all_gather(merger_scales, "ctx", axis=2, tiled=True)
    width = codes_piece.shape[2]
    dequant = (codes_piece.astype(jnp.float32) * scale_piece.astype(jnp.float32)).astype(
        jnp.bfloat16
    )
    product = jnp.dot(flat, dequant.reshape(-1, width), preferred_element_type=jnp.float32)
    mine = lax.psum_scatter(
        product.astype(jnp.bfloat16), "wt", scatter_dimension=1, tiled=True
    ).astype(jnp.float32)
    return (mine + merger_bias).astype(jnp.bfloat16)


def route_tokens(values, positions, span):
    owners = lax.axis_size("ctx")
    items = values.shape[0]
    capacity = 2 * positions.shape[0] // owners
    target = positions // span
    item_order = jnp.arange(items, dtype=jnp.int32)
    before = (target[None, :] == target[:, None]) & (item_order[None, :] < item_order[:, None])
    ranks = jnp.sum(before.astype(jnp.int32), axis=1)
    slots = target * capacity + ranks
    table = slots[None, :] == jnp.arange(owners * capacity, dtype=jnp.int32)[:, None]
    packed = jnp.dot(table.astype(jnp.bfloat16), values, preferred_element_type=jnp.float32).astype(
        jnp.bfloat16
    )
    labels = jnp.sum(jnp.where(table, positions[None, :] + 1, 0), axis=1) - 1
    return (
        lax.all_to_all(packed, "ctx", split_axis=0, concat_axis=0, tiled=True),
        lax.all_to_all(labels, "ctx", split_axis=0, concat_axis=0, tiled=True),
    )


def place_tokens(text_embed, arrived, labels, first):
    local = labels - first
    table = local[None, :] == jnp.arange(text_embed.shape[0], dtype=jnp.int32)[:, None]
    filled = jnp.dot(
        table.astype(jnp.bfloat16), arrived, preferred_element_type=jnp.float32
    ).astype(jnp.bfloat16)
    covered = jnp.any(table, axis=1)
    return jnp.where(covered[:, None], filled, text_embed)


def on_device(
    patches,
    vit_gain,
    vit_codes,
    vit_scales,
    vit_bias,
    window_ids,
    merger_codes,
    merger_scales,
    merger_bias,
    positions,
    text_embed,
    norm_gain,
    llm_codes,
    llm_scales,
    llm_bias,
    segments,
):
    row_count = text_embed.shape[0]
    first = lax.axis_index("ctx") * row_count
    normed_patches = vision_norm_rows(patches, vit_gain)
    vit_weight = (vit_codes.astype(jnp.float32) * vit_scales.astype(jnp.float32)[0]).astype(
        jnp.bfloat16
    )
    attended = window_attention(normed_patches, vit_weight, vit_bias, window_ids)
    token_count = positions.shape[0]
    features = attended.reshape(token_count, MERGE, -1)
    projected = merge_project(features, merger_codes, merger_scales, merger_bias)
    embedded, labels = route_tokens(projected, positions, row_count)
    hidden = place_tokens(text_embed, embedded, labels, first)
    values = hidden.astype(jnp.float32)
    squares = lax.psum(jnp.sum(values * values, axis=1), "wt")
    normed = (values * lax.rsqrt(squares[:, None] / D + RMS_EPS) * norm_gain).astype(jnp.bfloat16)
    local_rows = normed.shape[1]
    codes_piece = lax.all_gather(llm_codes, "ctx", axis=2, tiled=True)
    scale_piece = lax.all_gather(llm_scales, "ctx", axis=2, tiled=True)
    width = codes_piece.shape[2]
    dequant_piece = (codes_piece.astype(jnp.float32) * scale_piece.astype(jnp.float32)).astype(
        jnp.bfloat16
    )
    product = jnp.dot(
        normed, dequant_piece.reshape(local_rows, -1), preferred_element_type=jnp.float32
    )
    partial_value = product.reshape(row_count, KVH, width)
    triple = (
        lax.psum_scatter(
            partial_value.astype(jnp.bfloat16), "wt", scatter_dimension=1, tiled=True
        ).astype(jnp.float32)
        + llm_bias
    )
    cosine, sine = rope_tables(first, row_count)
    queries, keys_rot, values_cut = split_heads(triple, cosine, sine)
    own = (keys_rot, values_cut, segments)
    arrivals = [own]
    moving = own
    for distance in range(REACH):
        moving = passed_along((moving[0], moving[1], moving[2]), "ctx", 1)
        arrivals.append(moving)
    keys_all = jnp.concatenate([arrival[0] for arrival in arrivals], axis=0)
    values_all = jnp.concatenate([arrival[1] for arrival in arrivals], axis=0)
    key_segments = jnp.concatenate([arrival[2] for arrival in arrivals], axis=0)
    key_places = jnp.concatenate(
        [
            first - distance * row_count + jnp.arange(row_count, dtype=jnp.int32)
            for distance in range(REACH + 1)
        ],
        axis=0,
    )
    query_places = first + jnp.arange(row_count, dtype=jnp.int32)
    allowed = (
        (segments[:, None] == key_segments[None, :])
        & (key_places[None, :] <= query_places[:, None])
        & (key_places[None, :] >= 0)
    )
    outputs = []
    for group_index in range(queries.shape[1]):
        scores = jnp.einsum(
            "qjd,kd->jqk",
            queries[:, group_index],
            keys_all[:, group_index],
            preferred_element_type=jnp.float32,
        ) * HD ** (-0.5)
        softmaxed = softmax_rows(scores, allowed[None]).astype(jnp.bfloat16)
        blended = jnp.einsum(
            "jqk,kd->qjd", softmaxed, values_all[:, group_index], preferred_element_type=jnp.float32
        )
        outputs.append(blended.astype(jnp.bfloat16).reshape(row_count, -1))
    return jnp.concatenate(outputs, axis=1)


def solution(mesh):
    in_specs = (
        P("ctx", None),
        P(),
        P(None, None, "wt"),
        P("wt"),
        P(None, "wt"),
        P("ctx"),
        P(None, "wt", "ctx"),
        P(None, "wt", "ctx"),
        P("wt"),
        P("ctx"),
        P("ctx", "wt"),
        P("wt"),
        P("wt", None, "ctx"),
        P("wt", None, "ctx"),
        P("wt", None),
        P("ctx"),
    )
    out_specs = P("ctx", "wt")
    return jax.shard_map(
        on_device, mesh=mesh, in_specs=in_specs, out_specs=out_specs, check_vma=False
    )
```

profile of v0, /device:TPU:1, one launch (start us, length us, event | category | flops | bytes accessed | tf_op | source)
XLA Modules:
  0.0 853.0 jit_solution(12550410183688036739)
XLA Ops:
  7.3 8.3 copy.82
  16.6 6.4 add_convert_fusion
  24.2 5.5 fusion.104
  29.7 4.3 fusion.75
  34.7 2.1 reshape_reshape_reshape.3
  36.8 24.0 %all_gather.13 = bf16[1,1,8192]{2,1,0:T(2,128)(2,1)S(1)} all-gather(bf16[1,1,512]{2,1,0:T(2,128)(2,1)S(1)} %copy-done.10), channel_id=1, replica_groups=mesh['ctx'=16,'wt'=2] {'ctx'}, dimensions={2}, use_global_device_ids=true | all-gather | bytes 17408 | tf_op jit(solution)/shard_map/all_gather | solution.py:88
  60.9 158.2 %all-gather.3.cloned.1.call-done = bf16[4,640,8192]{2,1,0:T(8,128)(2,1)} async-done(((bf16[4,640,512]{2,1,0:T(8,128)(2,1)}), bf16[4,640,8192]{2,1,0:T(8,128)(2,1)}) %all-gather.3.cloned.1.call-update) | async-done | bytes 41943056 | tf_op jit(solution)/shard_map/all_gather | solution.py:87
  219.1 28.4 %multiply_convert_fusion.1 = bf16[4,640,8192]{2,1,0:T(8,128)(2,1)} fusion(bf16[4,640,8192]{2,1,0:T(8,128)(2,1)} %all-gather.3.cloned.1.call-done, f32[8192]{0:T(1024)S(1)} %bitcast.234), kind=kLoop, calls=%fused_computation.6 | loop fusion | flops 62914560 | bytes 83918848 | tf_op jit(solution)/shard_map/convert_element_type | solution.py:90
  247.4 17.2 %convolution_convert_fusion = bf16[128,8192]{1,0:T(8,128)(2,1)} fusion(bf16[128,2560]{1,0:T(8,128)(2,1)S(1)} %reshape_reshape_reshape.3, bf16[2560,8192]{1,0:T(8,128)(2,1)} %bitcast.224), kind=kOutput, calls=%fused_computation.45 | convolution fusion | flops 5369757696 | bytes 44695552 | tf_op jit(solution)/shard_map/dot_general | solution.py:93
  266.4 5.0 all-to-all-start
  271.4 24.8 %reduce-scatter.3.cloned.1.call-done = bf16[128,4096]{1,0:T(8,128)(2,1)} async-done(((bf16[128,8192]{1,0:T(8,128)(2,1)}), bf16[128,4096]{1,0:T(8,128)(2,1)}) %reduce-scatter.3.cloned.1.call-update) | async-done | bytes 1048592 | tf_op jit(solution)/shard_map/reduce_scatter | solution.py:94
  296.3 3.3 convolution_convert_fusion.2
  299.5 6.4 all-to-all-start.1
  306.1 87.5 %all_gather.15 = bf16[1,8,768]{1,0,2:T(2,128)(2,1)S(1)} all-gather(bf16[1,8,48]{1,0,2:T(2,128)(2,1)S(1)} %copy.88), channel_id=1, replica_groups=mesh['ctx'=16,'wt'=2] {'ctx'}, dimensions={2}, use_global_device_ids=true | all-gather | bytes 13056 | tf_op jit(solution)/shard_map/all_gather | solution.py:165
  394.4 4.9 fusion.29
  399.3 4.2 psum.7
  403.5 177.3 %all-gather.5.cloned.1.call-done = bf16[4096,8,768]{0,2,1:T(8,128)(2,1)} async-done(((bf16[4096,8,48]{0,2,1:T(8,128)(2,1)}), bf16[4096,8,768]{0,2,1:T(8,128)(2,1)}) %all-gather.5.cloned.1.call-update) | async-done | bytes 50331664 | tf_op jit(solution)/shard_map/all_gather | solution.py:164
  580.8 33.5 %fusion.48 = bf16[512,8,768]{2,0,1:T(8,128)(2,1)} fusion(bf16[4096,8,768]{0,2,1:T(8,128)(2,1)} %all-gather.5.cloned.1.call-done, f32[8,768]{1,0:T(8,128)S(1)} %copy.89, bf16[512,4096]{1,0:T(8,128)(2,1)} %get-tuple-element.25, f32[4096]{0:T(1024)S(1)} %copy-done.12, f32[512]{0:T(512)S(1)} %add_rsqrt_fusion), kind=kOutput, calls=%fused_computation.75 | convolution fusion | flops 25856835584 | bytes 60860416 | tf_op jit(solution)/shard_map/dot_general | solution.py:170
  614.9 3.4 collective-permute-start.4
  619.7 3.3 collective-permute-start.5
  623.8 13.5 %collective-permute-start.6 = (s32[512]{0:T(512)S(1)}, s32[512]{0:T(512)S(1)}, u32[]{:S(2)}, u32[]{:S(2)}) collective-permute-start(s32[512]{0:T(512)S(1)} %collective-permute-done.5), channel_id=1, source_target_pairs={{0,2},{2,4},{4,6},{6,8},{8,10},{10,12},{12,14},{14,16},{16,18},{18... | collective-permute-start | bytes 6152 | tf_op jit(solution)/shard_map/ppermute | solution.py:24
  637.9 4.2 collective-permute-start.7
  642.8 59.0 %reduce-scatter.5.cloned.1.call-done = bf16[512,4,768]{2,0,1:T(8,128)(2,1)} async-done(((bf16[512,8,768]{2,0,1:T(8,128)(2,1)}), bf16[512,4,768]{2,0,1:T(8,128)(2,1)}) %reduce-scatter.5.cloned.1.call-update) | async-done | bytes 3145744 | tf_op jit(solution)/shard_map/reduce_scatter | solution.py:175
  701.8 2.4 convert_add_fusion
  704.6 1.6 constant_dynamic-update-slice_fusion.4
  706.2 3.8 collective-permute-start.8
  710.0 1.9 collective-permute-start
  712.0 2.3 and_and_fusion
  716.1 4.4 collective-permute-start.9
  721.8 4.4 collective-permute-start.1
  727.6 4.2 collective-permute-start.10
  733.0 4.5 collective-permute-start.2
  737.5 2.5 fusion.41
  740.9 2.1 collective-permute-start.11
  743.9 1.9 constant_dynamic-update-slice_fusion.9
  745.8 1.9 constant_dynamic-update-slice_fusion.2
  747.8 4.5 collective-permute-start.3
  753.2 2.0 constant_dynamic-update-slice_fusion.1
  756.1 12.6 %fusion.108 = (f32[4,512]{1,0:T(4,128)S(1)}, f32[4,512,2560]{1,2,0:T(8,128)}) fusion(pred[512,2560]{0,1:T(8,128)(4,1)S(1)} %and_and_fusion, bf16[2560,4,128]{2,0,1:T(8,128)(2,1)} %constant_dynamic-update-slice_fusion.7, bf16[512,4,4,128]{3,0,2,1:T(8,128)(2,1)S(1)} %copy-done), kind=kOutput, calls=%fused_computation.183 | convolution fusion | flops 1363151360 | bytes 23470080 | tf_op jit(solution)/shard_map/sub | solution.py:30
  768.7 12.6 %fusion.107 = (f32[4,512]{1,0:T(4,128)S(1)}, f32[4,512,2560]{1,2,0:T(8,128)}) fusion(pred[512,2560]{0,1:T(8,128)(4,1)S(1)} %and_and_fusion, bf16[2560,4,128]{2,0,1:T(8,128)(2,1)} %constant_dynamic-update-slice_fusion.7, bf16[512,4,4,128]{3,0,2,1:T(8,128)(2,1)S(1)} %copy-done), kind=kOutput, calls=%fused_computation.182 | convolution fusion | flops 1363151360 | bytes 23470080 | tf_op jit(solution)/shard_map/sub | solution.py:30
  781.2 12.5 %fusion.106 = (f32[4,512]{1,0:T(4,128)S(1)}, f32[4,512,2560]{1,2,0:T(8,128)}) fusion(pred[512,2560]{0,1:T(8,128)(4,1)S(1)} %and_and_fusion, bf16[2560,4,128]{2,0,1:T(8,128)(2,1)} %constant_dynamic-update-slice_fusion.7, bf16[512,4,4,128]{3,0,2,1:T(8,128)(2,1)S(1)} %copy-done), kind=kOutput, calls=%fused_computation.181 | convolution fusion | flops 1363151360 | bytes 23470080 | tf_op jit(solution)/shard_map/sub | solution.py:30
  793.8 12.8 %fusion.105 = (f32[4,512]{1,0:T(4,128)S(1)}, f32[4,512,2560]{1,2,0:T(8,128)}) fusion(pred[512,2560]{0,1:T(8,128)(4,1)S(1)} %and_and_fusion, bf16[2560,4,128]{2,0,1:T(8,128)(2,1)} %constant_dynamic-update-slice_fusion.7, bf16[512,4,4,128]{3,0,2,1:T(8,128)(2,1)S(1)} %copy-done), kind=kOutput, calls=%fused_computation.180 | convolution fusion | flops 1363151360 | bytes 23470080 | tf_op jit(solution)/shard_map/sub | solution.py:30
  806.5 2.0 constant_dynamic-update-slice_fusion
  808.5 8.7 %fusion.74 = bf16[128,4,512]{2,0,1:T(8,128)(2,1)S(1)} fusion(f32[4,512,2560]{1,2,0:T(8,128)} %get-tuple-element.33, f32[4,512]{1,0:T(4,128)S(1)} %get-tuple-element.32, bf16[2560,4,128]{2,0,1:T(8,128)(2,1)} %constant_dynamic-update-slice_fusion), kind=kOutput, calls=%fused_computation.94 | convolution fusion | flops 1352925184 | bytes 22159360 | tf_op jit(solution)/shard_map/jqk,kd->qjd/dot_general | solution.py:213
  817.5 8.7 %fusion.73 = bf16[128,4,512]{2,0,1:T(8,128)(2,1)S(1)} fusion(f32[4,512,2560]{1,2,0:T(8,128)} %get-tuple-element.31, f32[4,512]{1,0:T(4,128)S(1)} %get-tuple-element.30, bf16[2560,4,128]{2,0,1:T(8,128)(2,1)} %constant_dynamic-update-slice_fusion), kind=kOutput, calls=%fused_computation.93 | convolution fusion | flops 1352925184 | bytes 22159360 | tf_op jit(solution)/shard_map/jqk,kd->qjd/dot_general | solution.py:213
  826.4 8.7 %fusion.72 = bf16[128,4,512]{2,0,1:T(8,128)(2,1)S(1)} fusion(f32[4,512,2560]{1,2,0:T(8,128)} %get-tuple-element.29, f32[4,512]{1,0:T(4,128)S(1)} %get-tuple-element.28, bf16[2560,4,128]{2,0,1:T(8,128)(2,1)} %constant_dynamic-update-slice_fusion), kind=kOutput, calls=%fused_computation.92 | convolution fusion | flops 1352925184 | bytes 22159360 | tf_op jit(solution)/shard_map/jqk,kd->qjd/dot_general | solution.py:213
  835.4 8.7 %fusion.71 = bf16[128,4,512]{2,0,1:T(8,128)(2,1)S(1)} fusion(f32[4,512,2560]{1,2,0:T(8,128)} %get-tuple-element.27, f32[4,512]{1,0:T(4,128)S(1)} %get-tuple-element.26, bf16[2560,4,128]{2,0,1:T(8,128)(2,1)} %constant_dynamic-update-slice_fusion), kind=kOutput, calls=%fused_computation.91 | convolution fusion | flops 1352925184 | bytes 22159360 | tf_op jit(solution)/shard_map/jqk,kd->qjd/dot_general | solution.py:213
  844.4 1.6 pad_maximum_fusion
  (104 shorter events, 20.4 us)
Async XLA Ops:
  6.5 212.5 %all-gather.3.cloned.1.call-start = ((), (), s32[]{:S(2)}) async-start(), calls=%async_computation.4 | async-start | bytes 44564480 | tf_op jit(solution)/shard_map/all_gather | solution.py:87
  7.3 9.0 %copy-start.1 = (bf16[512,1280]{1,0:T(8,128)(2,1)S(1)}, bf16[512,1280]{1,0:T(8,128)(2,1)}, u32[]{:S(2)}) copy-start(bf16[512,1280]{1,0:T(8,128)(2,1)} %param.16) | copy-start | bytes 3932164
  7.3 9.4 %copy-start.13 = (f32[3,640]{1,0:T(4,128)S(1)}, f32[3,640]{1,0:T(4,128)}, u32[]{:S(2)}) copy-start(f32[3,640]{1,0:T(4,128)} %param.20) | copy-start | bytes 23044
  7.3 9.4 %copy-start.14 = (f32[1280]{0:T(1024)S(1)}, f32[1280]{0:T(1024)}, u32[]{:S(2)}) copy-start(f32[1280]{0:T(1024)} %param.17) | copy-start | bytes 15364
  7.3 289.0 %reduce-scatter.3.cloned.1.call-start = ((), (), s32[]{:S(2)}) async-start(), calls=%async_computation.5 | async-start | bytes 3145728 | tf_op jit(solution)/shard_map/reduce_scatter | solution.py:94
  23.0 1.0 copy-start.8
  29.7 7.1 copy-start.10
  264.6 0.8 copy-start.15
  264.6 31.7 %copy-start.6 = (f32[4096]{0:T(1024)S(1)}, f32[4096]{0:T(1024)}, u32[]{:S(2)}) copy-start(f32[4096]{0:T(1024)} %param.24) | copy-start | bytes 49156
  264.6 316.2 %all-gather.5.cloned.1.call-start = ((), (), s32[]{:S(2)}) async-start(), calls=%async_computation.6 | async-start | bytes 53477376 | tf_op jit(solution)/shard_map/all_gather | solution.py:164
  265.4 40.6 %copy-start.11 = (bf16[1,8,48]{2,1,0:T(8,128)(2,1)S(1)}, bf16[1,8,48]{2,1,0:T(8,128)(2,1)}, u32[]{:S(2)}) copy-start(bf16[1,8,48]{2,1,0:T(8,128)(2,1)} %param.29) | copy-start | bytes 2308
  266.4 33.1 %all-to-all-start = ((s32[16,16,1]{1,2,0:T(1,128)}), s32[16,16,1]{1,2,0:T(1,128)S(1)}, u32[]{:S(2)}, u32[]{:S(2)}) async-start(s32[16,16,1]{1,2,0:T(1,128)} %bitcast), calls=%async_computation | async-start | bytes 16384 | tf_op jit(solution)/shard_map/all_to_all | solution.py:116
  299.5 94.9 %all-to-all-start.1 = ((bf16[16,16,4096]{2,1,0:T(8,128)(2,1)}), bf16[16,16,4096]{2,1,0:T(8,128)(2,1)S(1)}, u32[]{:S(2)}, u32[]{:S(2)}) async-start(bf16[16,16,4096]{2,1,0:T(8,128)(2,1)} %bitcast.12), calls=%async_computation.2 | async-start | bytes 4194304 | tf_op jit(solution)/shard_map/all_to_all | solution.py:115
  305.9 395.9 %reduce-scatter.5.cloned.1.call-start = ((), (), s32[]{:S(2)}) async-start(), calls=%async_computation.7 | async-start | bytes 9437184 | tf_op jit(solution)/shard_map/reduce_scatter | solution.py:175
  394.4 186.4 %copy-start.12 = (f32[4096]{0:T(1024)S(1)}, f32[4096]{0:T(1024)}, u32[]{:S(2)}) copy-start(f32[4096]{0:T(1024)} %param.27) | copy-start | bytes 49156
  614.3 0.7 copy-start.9
  614.3 87.5 %copy-start.7 = (f32[4,768]{1,0:T(4,128)S(1)}, f32[4,768]{1,0:T(4,128)}, u32[]{:S(2)}) copy-start(f32[4,768]{1,0:T(4,128)} %param.30) | copy-start | bytes 36868
  614.9 4.8 collective-permute-start.4
  619.7 4.0 collective-permute-start.5
  623.8 14.2 %collective-permute-start.6 = (s32[512]{0:T(512)S(1)}, s32[512]{0:T(512)S(1)}, u32[]{:S(2)}, u32[]{:S(2)}) collective-permute-start(s32[512]{0:T(512)S(1)} %collective-permute-done.5), channel_id=1, source_target_pairs={{0,2},{2,4},{4,6},{6,8},{8,10},{10,12},{12,14},{14,16},{16,18},{18... | collective-permute-start | bytes 6152 | tf_op jit(solution)/shard_map/ppermute | solution.py:24
  637.9 4.9 collective-permute-start.7
  706.2 9.9 %collective-permute-start.8 = (bf16[512,4,128]{2,0,1:T(8,128)(2,1)S(1)}, bf16[512,4,128]{2,0,1:T(8,128)(2,1)S(1)}, u32[]{:S(2)}, u32[]{:S(2)}) collective-permute-start(bf16[512,4,128]{2,0,1:T(8,128)(2,1)S(1)} %get-tuple-element.10), channel_id=1, source_target_pairs={{0,2},{2,4},{4,6},{6,8},{8,10},{10,12},{12,14},{14,16},{16,18},{18... | collective-permute-start | bytes 1572872 | tf_op jit(solution)/shard_map/ppermute | solution.py:24
  710.0 11.7 %collective-permute-start = (bf16[512,4,128]{2,0,1:T(8,128)(2,1)S(1)}, bf16[512,4,128]{2,0,1:T(8,128)(2,1)S(1)}, u32[]{:S(2)}, u32[]{:S(2)}) collective-permute-start(bf16[512,4,128]{2,0,1:T(8,128)(2,1)S(1)} %get-tuple-element.6), channel_id=1, source_target_pairs={{0,2},{2,4},{4,6},{6,8},{8,10},{10,12},{12,14},{14,16},{16,18},{18... | collective-permute-start | bytes 1572872 | tf_op jit(solution)/shard_map/ppermute | solution.py:24
  716.1 11.5 %copy-start.4 = (bf16[512,4,128]{2,0,1:T(8,128)(2,1)}, bf16[512,4,128]{2,0,1:T(8,128)(2,1)S(1)}, u32[]{:S(2)}) copy-start(bf16[512,4,128]{2,0,1:T(8,128)(2,1)S(1)} %collective-permute-done.8) | copy-start | bytes 1572868
  716.1 11.5 %collective-permute-start.9 = (bf16[512,4,128]{2,0,1:T(8,128)(2,1)S(1)}, bf16[512,4,128]{2,0,1:T(8,128)(2,1)}, u32[]{:S(2)}, u32[]{:S(2)}) collective-permute-start(bf16[512,4,128]{2,0,1:T(8,128)(2,1)S(1)} %collective-permute-done.8), channel_id=1, source_target_pairs={{0,2},{2,4},{4,6},{6,8},{8,10},{10,12},{12,14},{14,16},{16,18},{18... | collective-permute-start | bytes 1572872 | tf_op jit(solution)/shard_map/ppermute | solution.py:24
  721.8 5.9 copy-start.2
  721.8 11.2 %collective-permute-start.1 = (bf16[512,4,128]{2,0,1:T(8,128)(2,1)S(1)}, bf16[512,4,128]{2,0,1:T(8,128)(2,1)}, u32[]{:S(2)}, u32[]{:S(2)}) collective-permute-start(bf16[512,4,128]{2,0,1:T(8,128)(2,1)S(1)} %collective-permute-done), channel_id=1, source_target_pairs={{0,2},{2,4},{4,6},{6,8},{8,10},{10,12},{12,14},{14,16},{16,18},{18... | collective-permute-start | bytes 1572872 | tf_op jit(solution)/shard_map/ppermute | solution.py:24
  727.6 13.2 %collective-permute-start.10 = (bf16[512,4,128]{2,0,1:T(8,128)(2,1)}, bf16[512,4,128]{2,0,1:T(8,128)(2,1)S(1)}, u32[]{:S(2)}, u32[]{:S(2)}) collective-permute-start(bf16[512,4,128]{2,0,1:T(8,128)(2,1)} %collective-permute-done.9), channel_id=1, source_target_pairs={{0,2},{2,4},{4,6},{6,8},{8,10},{10,12},{12,14},{14,16},{16,18},{18... | collective-permute-start | bytes 1572872 | tf_op jit(solution)/shard_map/ppermute | solution.py:24
  733.0 14.8 %collective-permute-start.2 = (bf16[512,4,128]{2,0,1:T(8,128)(2,1)}, bf16[512,4,128]{2,0,1:T(8,128)(2,1)}, u32[]{:S(2)}, u32[]{:S(2)}) collective-permute-start(bf16[512,4,128]{2,0,1:T(8,128)(2,1)} %collective-permute-done.1), channel_id=1, source_target_pairs={{0,2},{2,4},{4,6},{6,8},{8,10},{10,12},{12,14},{14,16},{16,18},{18... | collective-permute-start | bytes 1572872 | tf_op jit(solution)/shard_map/ppermute | solution.py:24
  737.5 2.5 copy-start.5
  737.5 5.5 copy-start.3
  740.0 16.1 %copy-start = (bf16[512,4,4,128]{3,0,2,1:T(8,128)(2,1)S(1)}, bf16[512,4,4,128]{3,0,2,1:T(8,128)(2,1)}, u32[]{:S(2)}) copy-start(bf16[512,4,4,128]{3,0,2,1:T(8,128)(2,1)} %fusion.41) | copy-start | bytes 6291460
  740.9 14.3 %collective-permute-start.11 = (bf16[512,4,128]{2,0,1:T(8,128)(2,1)S(1)}, bf16[512,4,128]{2,0,1:T(8,128)(2,1)S(1)}, u32[]{:S(2)}, u32[]{:S(2)}) collective-permute-start(bf16[512,4,128]{2,0,1:T(8,128)(2,1)S(1)} %collective-permute-done.10), channel_id=1, source_target_pairs={{0,2},{2,4},{4,6},{6,8},{8,10},{10,12},{12,14},{14,16},{16,18},{18... | collective-permute-start | bytes 1572872 | tf_op jit(solution)/shard_map/ppermute | solution.py:24
  747.8 58.7 %collective-permute-start.3 = (bf16[512,4,128]{2,0,1:T(8,128)(2,1)}, bf16[512,4,128]{2,0,1:T(8,128)(2,1)}, u32[]{:S(2)}, u32[]{:S(2)}) collective-permute-start(bf16[512,4,128]{2,0,1:T(8,128)(2,1)} %collective-permute-done.2), channel_id=1, source_target_pairs={{0,2},{2,4},{4,6},{6,8},{8,10},{10,12},{12,14},{14,16},{16,18},{18... | collective-permute-start | bytes 1572872 | tf_op jit(solution)/shard_map/ppermute | solution.py:24
Sparse Core Ops, SparseCore 0:
  8.9 210.1 all-gather.2
  264.8 31.4 reduce-scatter.2
  297.8 282.9 all-gather.4
  614.4 87.3 reduce-scatter.4
where the time goes:
time: 861 us; the launch traced here: 853 us
  waiting for transfers between devices  427 us (50%)
  matrix products  160 us (19%)
  blocking collectives  116 us (13%)
  starting transfers between devices  65.6 us (8%)
  other arithmetic  43.4 us (5%)
  local copies, waits for them, and re-layouts  26.5 us (3%)
  between operations  14.8 us (2%)
    all_gather x1, waiting for transfers between devices, on_device(): codes_piece = lax.all_gather(llm_codes, 'ctx', axis=2, tiled=True)  177 us
    all_gather x1, waiting for transfers between devices, merge_project(): codes_piece = lax.all_gather(merger_codes, 'ctx', axis=2, tiled=True)  158 us
    all_gather x1, blocking collectives, on_device(): scale_piece = lax.all_gather(llm_scales, 'ctx', axis=2, tiled=True)  87.5 us
    reduce_scatter x1, waiting for transfers between devices, on_device(): lax.psum_scatter(partial_value.astype(jnp.bfloat16), 'wt', scatter_dimens...  59 us
    sub x5, matrix products, softmax_rows(): raised = jnp.exp(masked - highest)  55.9 us
    ppermute x12, starting transfers between devices, passed_along(): lax.ppermute(value, axis, [(source, source + steps) for source in range(l...  54.1 us
    dot_general x4, matrix products, on_device(): jnp.einsum('jqk,kd->qjd', softmaxed, values_all[:, group_index], preferre...  35 us
    dot_general x1, matrix products, on_device(): jnp.dot(normed, dequant_piece.reshape(local_rows, -1), preferred_element_...  33.5 us
  transfers between devices with their start and end apart: 18, of which 10 were waited for; matrix products, arithmetic and copies ran while one was open for 13% of the time, Pallas kernels for 0%

commit v1 on v0

v1 whole, which is shorter than its diff:
```python
import functools
import math

import jax
import jax.numpy as jnp
from jax import lax
from jax.experimental import pallas as pl
from jax.experimental.pallas import tpu as pltpu
from jax.sharding import PartitionSpec as P


VHD = 80
D = 8192
KVH = 8
HD = 128
GROUP = 4
REACH = 4


VIT_EPS = 1e-06
RMS_EPS = 1e-06
ROPE_BASE = 1000000.0
FILL_LOW = -1e30


def shifted(value, axis, steps):
    count = lax.axis_size(axis)
    return lax.ppermute(value, axis, [(i, (i + steps) % count) for i in range(count)])


def passed_along(value, axis, steps):
    count = lax.axis_size(axis)
    return lax.ppermute(value, axis, [(i, i + steps) for i in range(count - steps)])


def softmax_rows(scores, allowed):
    masked = jnp.where(allowed, scores, FILL_LOW)
    highest = jnp.max(masked, axis=-1, keepdims=True)
    raised = jnp.exp(masked - highest)
    return raised / jnp.sum(raised, axis=-1, keepdims=True)


def vision_norm_rows(patches, vit_gain):
    values = patches.astype(jnp.float32)
    mean_square = jnp.mean(values * values, axis=1, keepdims=True)
    return (values * lax.rsqrt(mean_square + VIT_EPS) * vit_gain).astype(jnp.bfloat16)


def window_attention(normed, weight_block, bias_block, window_ids):
    row_count = normed.shape[0]
    packed = jnp.dot(
        normed, weight_block.reshape(normed.shape[1], -1), preferred_element_type=jnp.float32
    )
    triple = (packed.reshape(row_count, 3, -1) + bias_block).astype(jnp.bfloat16)
    heads_here = triple.shape[2] // VHD
    queries = triple[:, 0].reshape(row_count, heads_here, VHD)
    keys_here = triple[:, 1].reshape(row_count, heads_here, VHD)
    values_here = triple[:, 2].reshape(row_count, heads_here, VHD)
    scores = jnp.einsum(
        "qhd,khd->hqk", queries, keys_here, preferred_element_type=jnp.float32
    ) * VHD ** (-0.5)
    allowed = window_ids[:, None] == window_ids[None, :]
    softmaxed = softmax_rows(scores, allowed[None]).astype(jnp.bfloat16)
    blended = jnp.einsum("hqk,khd->qhd", softmaxed, values_here, preferred_element_type=jnp.float32)
    return blended.astype(jnp.bfloat16).reshape(row_count, -1)


def rope_tables(first, length):
    places = (first + jnp.arange(length, dtype=jnp.int32)).astype(jnp.float32)
    frequency = ROPE_BASE ** (-jnp.arange(0, HD, 2).astype(jnp.float32) / HD)
    angles = places[:, None] * frequency[None, :]
    angles = jnp.concatenate([angles, angles], axis=1)
    return (jnp.cos(angles), jnp.sin(angles))


def chip_ring(chips):
    return [0] + list(range(1, chips, 2)) + list(range(chips - 2, 0, -2))


def gather_features(features, numbers):
    count = lax.axis_size("ctx")
    chips = count // 2
    ring = jnp.asarray(chip_ring(chips), jnp.int32)
    order = chip_ring(chips)
    where_on = [order.index(chip) for chip in range(chips)]
    me = lax.axis_index("ctx")
    core = me % 2
    spot = jnp.asarray(where_on, jnp.int32)[me // 2]
    pairs = []
    for at in range(chips):
        pairs.append((2 * order[at], 2 * order[(at + 1) % chips]))
        pairs.append((2 * order[at] + 1, 2 * order[(at - 1) % chips] + 1))
    swap = [(i, i ^ 1) for i in range(count)]
    rows = features.shape[0]
    partner = lax.ppermute(features, "ctx", swap)
    moving = jnp.concatenate([features, partner], axis=0)
    found = [(jnp.stack([me, me + 1 - 2 * core]), moving)]
    way = 1 - 2 * core
    small = lax.all_to_all(
        jnp.broadcast_to(numbers[None, :], (count, numbers.shape[0])),
        "ctx",
        split_axis=0,
        concat_axis=0,
        tiled=True,
    )
    for step in range(1, chips // 2 + 1):
        last = step == chips // 2
        sent = moving[:rows] if last else moving
        moving = lax.ppermute(sent, "ctx", pairs)
        other = lax.ppermute(moving, "ctx", swap)
        near = 2 * ring[(spot - way * step) % chips]
        far = 2 * ring[(spot + way * step) % chips]
        if last:
            found.append((jnp.stack([near + core]), moving))
            found.append((jnp.stack([far + 1 - core]), other))
        else:
            found.append((jnp.stack([near + core, near + 1 - core]), moving))
            found.append((jnp.stack([far + 1 - core, far + core]), other))
    return found, small


def summed_over_wt(parts):
    total = parts[0].astype(jnp.float32)
    for steps in range(1, len(parts)):
        arrived = shifted(parts[steps].astype(jnp.bfloat16), "wt", steps)
        total = total + arrived.astype(jnp.float32)
    return total


def turned_by_wt(pieces):
    count = len(pieces)
    here = lax.axis_index("wt")
    return [lax.select_n((here + k) % count, *pieces) for k in range(count)]


def finish_kernel(
    own_ref, arrived_ref, scale_ref, bias_ref, cosine_ref, sine_ref, *out_refs, rotated
):
    total = own_ref[...]
    for k in range(arrived_ref.shape[0]):
        total = total + arrived_ref[k].astype(jnp.float32)
    total = total * scale_ref[...] + bias_ref[...]
    factor = HD ** (-0.5) * math.log2(math.e)
    at = 0
    for out_ref in out_refs:
        for place in range(out_ref.shape[1] // HD):
            part = total[:, at * HD : (at + 1) * HD]
            if at < rotated:
                part = part * cosine_ref[...] + pltpu.roll(part, HD // 2, 1) * sine_ref[...]
            if at < GROUP:
                part = part * factor
            out_ref[:, place * HD : (place + 1) * HD] = part.astype(jnp.bfloat16)
            at += 1


def finish(own, arrived, row_scale, bias, cosine, sine, rotated, widths):
    rows, width = own.shape[0], sum(widths)
    tile = min(rows, 128)
    row = lambda columns: pl.BlockSpec((tile, columns), lambda i: (i, 0))
    return pl.pallas_call(
        functools.partial(finish_kernel, rotated=rotated),
        out_shape=tuple(jax.ShapeDtypeStruct((rows, cut), jnp.bfloat16) for cut in widths),
        grid=(rows // tile,),
        in_specs=[
            row(width),
            pl.BlockSpec((arrived.shape[0], tile, width), lambda i: (0, i, 0)),
            row(1),
            pl.BlockSpec((1, width), lambda i: (0, 0)),
            row(HD),
            row(HD),
        ],
        out_specs=tuple(row(cut) for cut in widths),
        cost_estimate=pl.CostEstimate(
            flops=20 * rows * width, transcendentals=0, bytes_accessed=12 * rows * width
        ),
        name="finish",
    )(own, arrived, row_scale, bias, cosine, sine)


def attend_kernel(need, q_ref, qseg_ref, kseg_ref, kv_ref, *refs, aliased):
    o_ref = refs[aliased]
    m_ref, l_ref, acc_ref, bar_ref, turned_ref = refs[aliased + 1 :]
    blocks, keys, _ = kv_ref.shape
    rows = q_ref.shape[0]

    def one_block(distance, start):
        same = kseg_ref[distance] == qseg_ref[...]
        if start:
            row = lax.broadcasted_iota(jnp.int32, (keys, rows), 1)
            column = lax.broadcasted_iota(jnp.int32, (keys, rows), 0)
            same = same & (column <= row)
        bar_ref[...] = jnp.where(same, 0.0, FILL_LOW)
        turned_ref[...] = jnp.transpose(kv_ref[distance, :, HD:])

        def one_head(head):
            query = q_ref[:, pl.ds(pl.multiple_of(head * HD, HD), HD)]
            scores = (
                lax.dot_general(
                    kv_ref[distance, :, :HD],
                    query,
                    (((1,), (1,)), ((), ())),
                    preferred_element_type=jnp.float32,
                )
                + bar_ref[...]
            )
            highest = jnp.max(scores, axis=0, keepdims=True)
            if not start:
                before = m_ref[head]
                highest = jnp.maximum(before, highest)
                fade = jnp.exp2(before - highest)
            raised = jnp.exp2(scores - highest)
            total = jnp.sum(raised, axis=0, keepdims=True)
            blended = jnp.dot(
                turned_ref[...], raised.astype(jnp.bfloat16), preferred_element_type=jnp.float32
            )
            if not start:
                total = l_ref[head] * fade + total
                blended = acc_ref[head] * fade + blended
            m_ref[head] = highest
            l_ref[head] = total
            acc_ref[head] = blended

        @pl.loop(0, GROUP // 2)
        def _(couple):
            one_head(2 * couple)
            one_head(2 * couple + 1)

    one_block(0, True)

    @pl.loop(1, blocks)
    def _(distance):
        pl.when(need[distance] > 0)(lambda: one_block(distance, False))

    for head in range(GROUP):
        o_ref[:, head * HD : (head + 1) * HD] = jnp.transpose(acc_ref[head] / l_ref[head]).astype(
            o_ref.dtype
        )


def attend(queries, pieces, query_segments, key_segments, need, group, groups, so_far):
    rows, width = queries.shape
    blocks, keys, _ = pieces.shape
    fixed = lambda shape: pl.BlockSpec(shape, lambda i, *_: (0,) * len(shape))
    aliased = 0 if so_far is None else 1
    return pl.pallas_call(
        functools.partial(attend_kernel, aliased=aliased),
        out_shape=jax.ShapeDtypeStruct((rows, width * groups), jnp.bfloat16),
        grid_spec=pltpu.PrefetchScalarGridSpec(
            num_scalar_prefetch=1,
            grid=(1,),
            in_specs=[
                fixed(queries.shape),
                fixed(query_segments.shape),
                fixed(key_segments.shape),
                fixed(pieces.shape),
            ]
            + [pl.BlockSpec(memory_space=pl.ANY)] * aliased,
            out_specs=pl.BlockSpec((rows, width), lambda i, *_: (0, group)),
            scratch_shapes=[
                pltpu.VMEM((GROUP, 1, rows), jnp.float32),
                pltpu.VMEM((GROUP, 1, rows), jnp.float32),
                pltpu.VMEM((GROUP, HD, rows), jnp.float32),
                pltpu.VMEM((keys, rows), jnp.float32),
                pltpu.VMEM((HD, keys), jnp.bfloat16),
            ],
        ),
        input_output_aliases={5: 0} if aliased else {},
        cost_estimate=pl.CostEstimate(
            flops=4 * rows * width * keys * blocks,
            transcendentals=rows * keys * blocks * GROUP,
            bytes_accessed=2 * rows * width * 4,
        ),
        name="attend",
    )(need, queries, query_segments, key_segments, pieces, *([so_far] * aliased))


def on_device(
    patches,
    vit_gain,
    vit_codes,
    vit_scales,
    vit_bias,
    window_ids,
    merger_codes,
    merger_scales,
    merger_bias,
    positions,
    text_embed,
    norm_gain,
    llm_codes,
    llm_scales,
    llm_bias,
    segments,
):
    row_count, local_rows = text_embed.shape
    owners = lax.axis_size("ctx")
    shares = lax.axis_size("wt")
    me = lax.axis_index("ctx")
    first = me * row_count
    groups_here = KVH // shares

    weight = jnp.transpose(llm_codes, (1, 2, 0)).astype(jnp.float32)
    weight = weight * llm_scales[0].astype(jnp.float32)[:, :, None] * norm_gain[None, None, :]
    weight = weight.astype(jnp.bfloat16)
    turned = jnp.stack(
        turned_by_wt([weight[k * groups_here : (k + 1) * groups_here] for k in range(shares)]),
        axis=1,
    )
    normed_patches = vision_norm_rows(patches, vit_gain)
    vit_weight = (vit_codes.astype(jnp.float32) * vit_scales.astype(jnp.float32)[0]).astype(
        jnp.bfloat16
    )
    attended = window_attention(normed_patches, vit_weight, vit_bias, window_ids)
    token_count = positions.shape[0]
    features = attended.reshape(token_count, -1)

    merger_weight = (merger_codes.astype(jnp.float32) * merger_scales.astype(jnp.float32)).astype(
        jnp.bfloat16
    )
    columns = merger_weight.shape[2]
    merger_weight = merger_weight.reshape(-1, columns)
    found, small = gather_features(features, jnp.concatenate([positions, segments]))
    all_positions = small[:, :token_count]
    all_segments = small[:, token_count:]
    early = max(1, groups_here - 1)
    gathered = [lax.all_gather(turned[:early], "ctx", axis=2, tiled=True)]
    sources = jnp.concatenate([source for source, _ in found])
    products = jnp.concatenate(
        [jnp.dot(rows, merger_weight, preferred_element_type=jnp.float32) for _, rows in found],
        axis=0,
    )
    part = columns // shares
    merged = summed_over_wt(
        turned_by_wt([products[:, k * part : (k + 1) * part] for k in range(shares)])
    ).astype(jnp.bfloat16)

    capacity = 2 * token_count // owners
    slots_each = owners * capacity
    target = all_positions // row_count
    item = jnp.arange(token_count, dtype=jnp.int32)
    before = (target[:, None, :] == target[:, :, None]) & (item[None, None, :] < item[None, :, None])
    ranks = jnp.sum(before.astype(jnp.int32), axis=2)
    slots = (
        target * slots_each + jnp.arange(owners, dtype=jnp.int32)[:, None] * capacity + ranks
    )
    slots_found = jnp.take(slots, sources, axis=0).reshape(-1)
    table = slots_found[None, :] == jnp.arange(owners * slots_each, dtype=jnp.int32)[:, None]
    mine = slots.reshape(1, -1) == me * slots_each + jnp.arange(slots_each, dtype=jnp.int32)[:, None]
    labels = jnp.sum(jnp.where(mine, all_positions.reshape(1, -1) + 1, 0), axis=1) - 1 - first
    place = labels[None, :] == jnp.arange(row_count, dtype=jnp.int32)[:, None]
    covered = jnp.any(place, axis=1)[:, None]
    table, place, covered = lax.optimization_barrier(
        (table.astype(jnp.bfloat16), place.astype(jnp.bfloat16), covered.astype(jnp.float32))
    )
    packed = jnp.dot(table, merged, preferred_element_type=jnp.float32).astype(jnp.bfloat16)
    arrived = lax.all_to_all(
        packed.reshape(owners, slots_each, part), "ctx", split_axis=0, concat_axis=0, tiled=True
    )
    if early < groups_here:
        late, arrived = lax.optimization_barrier((turned[early:], arrived))
        gathered.append(lax.all_gather(late, "ctx", axis=2, tiled=True))
    ours = turned_by_wt([block for block in arrived.reshape(shares, -1, slots_each, part)])
    held = [ours[0]] + [shifted(ours[k], "wt", k) for k in range(1, shares)]
    here = lax.axis_index("wt")
    whole_columns = jnp.concatenate(
        [lax.select_n((here - k) % shares, *held) for k in range(shares)], axis=2
    )
    flat = jnp.transpose(whole_columns, (1, 0, 2)).reshape(slots_each, -1)
    filled = jnp.dot(place, flat, preferred_element_type=jnp.float32)
    hidden = lax.optimization_barrier(
        jnp.where(covered > 0, (filled + merger_bias).astype(jnp.bfloat16), text_embed)
    )
    values = hidden.astype(jnp.float32)
    share = jnp.sum(values * values, axis=1)
    squares = share + sum(shifted(share, "wt", k) for k in range(1, shares))
    row_scale = lax.rsqrt(squares[:, None] / D + RMS_EPS)

    cosine, sine = rope_tables(first, row_count)
    sine = jnp.where(jnp.arange(HD) < HD // 2, -sine, sine)
    blocks = REACH + 1
    shards = me - jnp.arange(blocks, dtype=jnp.int32)
    key_segments = jnp.take(all_segments, jnp.maximum(shards, 0), axis=0)
    need = ((shards >= 0) & (key_segments[:, -1] >= segments[0])).astype(jnp.int32)
    query_segments = segments[None, :]
    key_segments = key_segments[:, :, None]
    ends = GROUP * HD
    full = ends + 2 * HD
    output = None
    for group in range(groups_here):
        held_at, at = (gathered[0], group) if group < early else (gathered[1], group - early)

        if group > 0:
            if group < early:
                held_at, product = lax.optimization_barrier((held_at, product))
                gathered[0] = held_at
            else:
                hidden, pieces = lax.optimization_barrier((hidden, pieces))
        if group > 0:
            output = attend(
                queries, pieces, query_segments, key_segments, need, group - 1, groups_here, output
            )
        columns_here = held_at[at].reshape(shares * full, local_rows)
        product = lax.dot_general(
            hidden, columns_here, (((1,), (1,)), ((), ())), preferred_element_type=jnp.float32
        )
        if group == 0:
            product, row_scale = lax.optimization_barrier((product, row_scale))
        arrived = jnp.stack(
            [
                shifted(product[:, k * full : (k + 1) * full].astype(jnp.bfloat16), "wt", k)
                for k in range(1, shares)
            ]
        )
        queries, pair = finish(
            product,
            arrived,
            row_scale,
            llm_bias[group][None, :],
            cosine,
            sine,
            GROUP + 1,
            [ends, 2 * HD],
        )
        pieces = jnp.stack(
            [pair] + [passed_along(pair, "ctx", distance) for distance in range(1, blocks)]
        )
    output = attend(
        queries, pieces, query_segments, key_segments, need, group, groups_here, output
    )
    return output


def solution(mesh):
    in_specs = (
        P("ctx", None),
        P(),
        P(None, None, "wt"),
        P("wt"),
        P(None, "wt"),
        P("ctx"),
        P(None, "wt", "ctx"),
        P(None, "wt", "ctx"),
        P("wt"),
        P("ctx"),
        P("ctx", "wt"),
        P("wt"),
        P("wt", None, "ctx"),
        P("wt", None, "ctx"),
        P("wt", None),
        P("ctx"),
    )
    out_specs = P("ctx", "wt")

    return jax.shard_map(
        on_device, mesh=mesh, in_specs=in_specs, out_specs=out_specs, check_vma=False
    )
```

time: 861 us -> 592 us (0.69)
  the two profiles are of different devices: /device:TPU:1 before, /device:TPU:27 now
where the time goes in v1:
time: 592 us; the launch traced here: 582 us
  waiting for transfers between devices  280 us (47%)
  matrix products  73.9 us (12%)
  local copies, waits for them, and re-layouts  65.1 us (11%)
  Pallas kernels  60.1 us (10%)
  starting transfers between devices  49.1 us (8%)
  other arithmetic  28.3 us (5%)
  between operations  25.2 us (4%)
    ppermute x4, waiting for transfers between devices, gather_features(): moving = lax.ppermute(sent, 'ctx', pairs)  103 us
    ppermute x7, waiting for transfers between devices, shifted(): lax.ppermute(value, axis, [(i, (i + steps) % count) for i in range(count)])  63 us
    all_to_all x1, waiting for transfers between devices, on_device(): lax.all_to_all(packed.reshape(owners, slots_each, part), 'ctx', split_axi...  44.3 us
    pallas_call x4, Pallas kernels, attend(): pl.pallas_call(functools.partial(attend_kernel, aliased=aliased), out_sha...  43.6 us
    ppermute x16, waiting for transfers between devices, passed_along(): lax.ppermute(value, axis, [(i, i + steps) for i in range(count - steps)])  43.5 us
    dot_general x4, matrix products, on_device(): lax.dot_general(hidden, columns_here, (((1,), (1,)), ((), ())), preferred...  35.9 us
    unnamed x83, local copies, waits for them, and re-layouts  31.8 us
    all_to_all x1, waiting for transfers between devices, gather_features(): lax.all_to_all(jnp.broadcast_to(numbers[None, :], (count, numbers.shape[0...  25 us
  transfers between devices with their start and end apart: 36, of which 18 were waited for; matrix products, arithmetic and copies ran while one was open for 23% of the time, Pallas kernels for 8%

profile of v1, /device:TPU:27, one launch (start us, length us, event | category | flops | bytes accessed | tf_op | source)
XLA Modules:
  0.0 582.2 jit_solution(12315778872411948975)
XLA Ops:
  7.2 2.9 fusion.12
  13.6 8.3 %copy.50 = bf16[1280,3,640]{0,2,1:T(8,128)(2,1)} copy(bf16[1280,3,640]{2,0,1:T(8,128)(2,1)} %param.20) | data formatting | bytes 9830400 | tf_op args[2]
  23.0 5.7 add_convert_fusion.1
  29.9 5.5 fusion.40
  35.5 4.5 fusion.23
  40.8 2.1 reshape_reshape.3
  46.9 44.6 %collective-permute-done.1 = bf16[256,2560]{1,0:T(8,128)(2,1)} collective-permute-done((bf16[256,2560]{1,0:T(8,128)(2,1)S(1)}, bf16[256,2560]{1,0:T(8,128)(2,1)}, u32[]{:S(2)}, u32[]{:S(2)}) %collective-permute-start.1) | collective-permute-done | bytes 1310752 | tf_op jit(solution)/shard_map/ppermute | solution.py:109
  92.6 7.6 %all-to-all-start = ((s32[16,1,640]{2,1,0:T(1,128)}), s32[16,1,640]{2,1,0:T(1,128)S(1)}, u32[]{:S(2)}, u32[]{:S(2)}) async-start(s32[16,1,640]{2,1,0:T(1,128)} %broadcast_in_dim.97), calls=%async_computation | async-start | bytes 81920 | tf_op jit(solution)/shard_map/all_to_all | solution.py:99
  111.8 2.4 multiply_convert_fusion.2
  114.3 25.0 %all-to-all-done = s32[16,1,640]{2,1,0:T(1,128)S(1)} async-done(((s32[16,1,640]{2,1,0:T(1,128)}), s32[16,1,640]{2,1,0:T(1,128)S(1)}, u32[]{:S(2)}, u32[]{:S(2)}) %all-to-all-start) | async-done | bytes 40992 | tf_op jit(solution)/shard_map/all_to_all | solution.py:99
  142.5 2.2 convolution_dynamic-update-slice_fusion.6
  144.7 2.1 convolution_dynamic-update-slice_fusion.5
  146.9 37.9 %collective-permute-done.5 = bf16[256,2560]{1,0:T(8,128)(2,1)} collective-permute-done((bf16[256,2560]{1,0:T(8,128)(2,1)}, bf16[256,2560]{1,0:T(8,128)(2,1)}, u32[]{:S(2)}, u32[]{:S(2)}) %collective-permute-start.5) | collective-permute-done | bytes 1310752 | tf_op jit(solution)/shard_map/ppermute | solution.py:109
  186.0 2.2 convolution_dynamic-update-slice_fusion.4
  190.1 2.1 convolution_dynamic-update-slice_fusion.3
  193.1 20.3 %collective-permute-done.7 = bf16[128,2560]{1,0:T(8,128)(2,1)S(1)} collective-permute-done((bf16[128,2560]{1,0:T(8,128)(2,1)S(1)}, bf16[128,2560]{1,0:T(8,128)(2,1)S(1)}, u32[]{:S(2)}, u32[]{:S(2)}) %collective-permute-start.7) | collective-permute-done | bytes 655392 | tf_op jit(solution)/shard_map/ppermute | solution.py:109
  214.1 2.1 convolution_dynamic-update-slice_fusion.1
  219.6 9.0 %fusion.1 = bf16[4096,2048]{1,0:T(8,128)(2,1)S(1)} fusion(s32[2048]{0:T(1024)S(1)} %select_bitcast_fusion.2), kind=kLoop, calls=%fused_computation.4 | loop fusion | flops 16777216 | bytes 16785408 | tf_op jit(solution)/shard_map/convert_element_type | solution.py:353
  229.2 14.0 %collective-permute-done.9 = bf16[2048,256]{1,0:T(8,128)(2,1)S(1)} collective-permute-done((bf16[2048,256]{1,0:T(8,128)(2,1)S(1)}, bf16[2048,256]{1,0:T(8,128)(2,1)S(1)}, u32[]{:S(2)}, u32[]{:S(2)}) %collective-permute-start.9) | collective-permute-done | bytes 1048608 | tf_op jit(solution)/shard_map/ppermute | solution.py:28
  243.2 7.5 %convolution_convert_fusion = bf16[4096,256]{1,0:T(8,128)(2,1)S(1)} fusion(bf16[4096,2048]{1,0:T(8,128)(2,1)S(1)} %fusion.1, bf16[2048,256]{1,0:T(8,128)(2,1)S(1)} %collective-permute-done.9, f32[2048,512]{1,0:T(8,128)} %copy-done.9, pred[]{:T(512)S(6)} %select_n.243), kind=kOutput, calls=%fused_computation.14 | convolution fusion | flops 4298113024 | bytes 24117248 | tf_op jit(solution)/shard_map/dot_general | solution.py:355
  250.6 2.4 copy.56
  253.0 6.5 %all-to-all-start.1 = ((bf16[16,256,256]{1,2,0:T(8,128)(2,1)}), bf16[16,256,256]{1,2,0:T(8,128)(2,1)S(1)}, u32[]{:S(2)}, u32[]{:S(2)}) async-start(bf16[16,256,256]{1,2,0:T(8,128)(2,1)} %copy.56), calls=%async_computation.1 | async-start | bytes 4194304 | tf_op jit(solution)/shard_map/all_to_all | solution.py:356
  259.6 2.1 pad_maximum_fusion.2
  261.7 44.3 %all-to-all-done.1 = bf16[16,256,256]{1,2,0:T(8,128)(2,1)S(1)} async-done(((bf16[16,256,256]{1,2,0:T(8,128)(2,1)}), bf16[16,256,256]{1,2,0:T(8,128)(2,1)S(1)}, u32[]{:S(2)}, u32[]{:S(2)}) %all-to-all-start.1) | async-done | bytes 2097184 | tf_op jit(solution)/shard_map/all_to_all | solution.py:356
  310.3 20.6 %collective-permute-done.10 = bf16[8,256,256]{1,2,0:T(8,128)(2,1)} collective-permute-done((bf16[8,256,256]{1,2,0:T(8,128)(2,1)S(1)}, bf16[8,256,256]{1,2,0:T(8,128)(2,1)}, u32[]{:S(2)}, u32[]{:S(2)}) %collective-permute-start.10) | collective-permute-done | bytes 1048608 | tf_op jit(solution)/shard_map/ppermute | solution.py:28
  341.8 4.7 slice-done
  348.0 6.7 %fusion.41.own_ref = f32[512,1536]{1,0:T(8,128)S(1)} fusion(bf16[512,4096]{1,0:T(8,128)(2,1)S(1)} %copy-done.7, bf16[1536,4096]{1,0:T(8,128)(2,1)S(1)} %bitcast.175), kind=kOutput, calls=%fused_computation.136 | convolution fusion | flops 6442450944 | bytes 19922944 | tf_op jit(solution)/shard_map/dot_general | solution.py:403
  354.7 5.8 slice-done.1
  360.5 9.0 %fusion.42.own_ref = f32[512,1536]{1,0:T(8,128)S(1)} fusion(bf16[512,4096]{1,0:T(8,128)(2,1)} %copy-done.6, bf16[1536,4096]{1,0:T(8,128)(2,1)S(1)} %bitcast.176), kind=kOutput, calls=%fused_computation.137 | convolution fusion | flops 6442450944 | bytes 19922944 | tf_op jit(solution)/shard_map/dot_general | solution.py:403
  371.5 4.0 slice-done.2
  375.5 9.5 %fusion.43.own_ref = f32[512,1536]{1,0:T(8,128)S(1)} fusion(bf16[512,4096]{1,0:T(8,128)(2,1)} %copy-done.6, bf16[1536,4096]{1,0:T(8,128)(2,1)S(1)} %bitcast.177), kind=kOutput, calls=%fused_computation.138 | convolution fusion | flops 6442450944 | bytes 19922944 | tf_op jit(solution)/shard_map/dot_general | solution.py:403
  396.2 9.1 %collective-permute-done.12 = bf16[512,768]{1,0:T(8,128)(2,1)} collective-permute-done((bf16[512,768]{1,0:T(8,128)(2,1)}, bf16[512,768]{1,0:T(8,128)(2,1)}, u32[]{:S(2)}, u32[]{:S(2)}) %collective-permute-start.12) | collective-permute-done | bytes 786464 | tf_op jit(solution)/shard_map/ppermute | solution.py:28
  405.3 4.1 finish.4
  413.4 8.7 %collective-permute-done.22 = bf16[512,768]{1,0:T(8,128)(2,1)} collective-permute-done((bf16[512,768]{1,0:T(8,128)(2,1)}, bf16[512,768]{1,0:T(8,128)(2,1)}, u32[]{:S(2)}, u32[]{:S(2)}) %collective-permute-start.22) | collective-permute-done | bytes 786464 | tf_op jit(solution)/shard_map/ppermute | solution.py:28
  423.4 4.1 finish.6
  429.9 8.9 %collective-permute-done.27 = bf16[512,768]{1,0:T(8,128)(2,1)S(1)} collective-permute-done((bf16[512,768]{1,0:T(8,128)(2,1)}, bf16[512,768]{1,0:T(8,128)(2,1)S(1)}, u32[]{:S(2)}, u32[]{:S(2)}) %collective-permute-start.27) | collective-permute-done | bytes 786464 | tf_op jit(solution)/shard_map/ppermute | solution.py:28
  440.2 4.1 finish.7
  454.1 10.7 %fusion.44.own_ref = f32[512,1536]{1,0:T(8,128)S(1)} fusion(bf16[512,4096]{1,0:T(8,128)(2,1)} %copy-done.6, bf16[1536,4096]{1,0:T(8,128)(2,1)} %bitcast.205), kind=kOutput, calls=%fused_computation.139 | convolution fusion | flops 6442450944 | bytes 19922944 | tf_op jit(solution)/shard_map/dot_general | solution.py:403
  476.3 2.1 collective-permute-done.29
  478.5 4.1 collective-permute-done.30
  482.6 10.2 %collective-permute-done.31 = bf16[512,256]{1,0:T(8,128)(2,1)S(1)} collective-permute-done((bf16[512,256]{1,0:T(8,128)(2,1)S(1)}, bf16[512,256]{1,0:T(8,128)(2,1)S(1)}, u32[]{:S(2)}, u32[]{:S(2)}) %collective-permute-start.31) | collective-permute-done | bytes 262176 | tf_op jit(solution)/shard_map/ppermute | solution.py:33
  493.9 11.0 %attend.4.refs_0_ = bf16[512,2048]{1,0:T(8,128)(2,1)} custom-call(s32[5]{0:T(128)} %and_convert_fusion.need, bf16[512,512]{1,0:T(8,128)(2,1)} %get-tuple-element.41.q_ref, s32[1,512]{1,0:T(1,128)} %bitcast.201, s32[5,512,1]{2,1,0:T(8,128)} %broadcast_select_fusion.4.kseg_ref, bf16[5,512,256]{2,1,0:T(8,128)(2,1)} %copy-done.17), custom_call_target="tpu_custom_call" | custom-call | flops 2684354560 | bytes 2097152 | tf_op jit(solution)/shard_map/attend/pallas_call | solution.py:245
  504.9 10.8 %attend.5.refs_0_ = bf16[512,2048]{1,0:T(8,128)(2,1)} custom-call(s32[5]{0:T(128)} %and_convert_fusion.need, bf16[512,512]{1,0:T(8,128)(2,1)} %get-tuple-element.39.q_ref, s32[1,512]{1,0:T(1,128)} %bitcast.202, s32[5,512,1]{2,1,0:T(8,128)} %broadcast_select_fusion.4.kseg_ref, bf16[5,512,256]{2,1,0:T(8,128)(2,1)} %copy-done.19, ...), custom_call_target="tpu_custom_call", output_to_operand_aliasing={{}: (5, {})} | custom-call | flops 2684354560 | bytes 2097152 | tf_op jit(solution)/shard_map/attend/pallas_call | solution.py:245
  515.7 4.1 finish.5
  521.1 11.0 %attend.6.refs_0_ = bf16[512,2048]{1,0:T(8,128)(2,1)} custom-call(s32[5]{0:T(128)} %and_convert_fusion.need, bf16[512,512]{1,0:T(8,128)(2,1)} %get-tuple-element.37.q_ref, s32[1,512]{1,0:T(1,128)} %bitcast.203, s32[5,512,1]{2,1,0:T(8,128)} %broadcast_select_fusion.4.kseg_ref, ...), custom_call_target="tpu_custom_call", output_to_operand_aliasing={{}: (5, {})} | custom-call | flops 2684354560 | bytes 2097152 | tf_op jit(solution)/shard_map/attend/pallas_call | solution.py:245
  536.0 16.3 %collective-permute-done.19 = bf16[512,256]{1,0:T(8,128)(2,1)S(1)} collective-permute-done((bf16[512,256]{1,0:T(8,128)(2,1)S(1)}, bf16[512,256]{1,0:T(8,128)(2,1)S(1)}, u32[]{:S(2)}, u32[]{:S(2)}) %collective-permute-start.19) | collective-permute-done | bytes 262176 | tf_op jit(solution)/shard_map/ppermute | solution.py:33
  553.4 9.9 %collective-permute-done.21 = bf16[512,256]{1,0:T(8,128)(2,1)S(1)} collective-permute-done((bf16[512,256]{1,0:T(8,128)(2,1)S(1)}, bf16[512,256]{1,0:T(8,128)(2,1)S(1)}, u32[]{:S(2)}, u32[]{:S(2)}) %collective-permute-start.21) | collective-permute-done | bytes 262176 | tf_op jit(solution)/shard_map/ppermute | solution.py:33
  564.4 10.8 %attend.7 = bf16[512,2048]{1,0:T(8,128)(2,1)} custom-call(s32[5]{0:T(128)} %and_convert_fusion.need, bf16[512,512]{1,0:T(8,128)(2,1)} %get-tuple-element.35.q_ref, s32[1,512]{1,0:T(1,128)} %bitcast.204, s32[5,512,1]{2,1,0:T(8,128)} %broadcast_select_fusion.4.kseg_ref, bf16[5,512,256]{2,1,0:T(8,128)(2,1)} %copy-done.20, ...), custom_call_target="tpu_custom_call", output_to_operand_aliasing={{}: (5, {})} | custom-call | flops 2684354560 | bytes 2097152 | tf_op jit(solution)/shard_map/attend/pallas_call | solution.py:245
  (214 shorter events, 93.3 us)
Async XLA Ops:
  6.5 335.3 %all-gather.3.cloned.1.call-start = ((), (), s32[]{:S(2)}) async-start(), calls=%async_computation.2 | async-start | bytes 40108032 | tf_op jit(solution)/shard_map/all_gather | solution.py:326
  39.9 52.0 %copy-start.25 = (s32[512]{0:T(512)S(1)}, s32[512]{0:T(512)}, u32[]{:S(2)}) copy-start(s32[512]{0:T(512)} %param.33) | copy-start | bytes 6148
  40.0 52.0 %copy-start.26 = (s32[128]{0:T(128)S(1)}, s32[128]{0:T(128)}, u32[]{:S(2)}) copy-start(s32[128]{0:T(128)} %param.27) | copy-start | bytes 1540
  40.7 59.5 %copy-start.31 = (s32[8]{0:T(128)S(1)}, s32[8]{0:T(128)}, u32[]{:S(2)}) copy-start(s32[8]{0:T(128)} %constant.193.clone) | copy-start | bytes 100
  40.7 65.1 %copy-start.21 = (s32[8]{0:T(128)S(1)}, s32[8]{0:T(128)}, u32[]{:S(2)}) copy-start(s32[8]{0:T(128)} %constant.192.clone) | copy-start | bytes 100
  40.7 70.8 %copy-start.24 = (bf16[1,1,512]{2,1,0:T(2,128)(2,1)S(1)}, bf16[1,1,512]{2,1,0:T(2,128)(2,1)}, u32[]{:S(2)}) copy-start(bf16[1,1,512]{2,1,0:T(2,128)(2,1)} %param.25) | copy-start | bytes 3076
  42.8 2.5 collective-permute-start
  46.4 45.1 %collective-permute-start.1 = (bf16[256,2560]{1,0:T(8,128)(2,1)S(1)}, bf16[256,2560]{1,0:T(8,128)(2,1)}, u32[]{:S(2)}, u32[]{:S(2)}) collective-permute-start(bf16[256,2560]{1,0:T(8,128)(2,1)S(1)} %constant_dynamic-update-slice_fusion), channel_id=1, source_target_pairs={{0,4},{2,10},{4,12},{6,2},{12,20},{14,6},{20,28},{22,14},{28,24},{... | collective-permute-start | bytes 3932168 | tf_op jit(solution)/shard_map/ppermute | solution.py:109
  91.5 48.0 %collective-permute-start.3 = (bf16[256,2560]{1,0:T(8,128)(2,1)}, bf16[256,2560]{1,0:T(8,128)(2,1)}, u32[]{:S(2)}, u32[]{:S(2)}) collective-permute-start(bf16[256,2560]{1,0:T(8,128)(2,1)} %collective-permute-done.1), channel_id=1, source_target_pairs={{0,4},{2,10},{4,12},{6,2},{12,20},{14,6},{20,28},{22,14},{28,24},{... | collective-permute-start | bytes 3932168 | tf_op jit(solution)/shard_map/ppermute | solution.py:109
  92.6 46.7 %all-to-all-start = ((s32[16,1,640]{2,1,0:T(1,128)}), s32[16,1,640]{2,1,0:T(1,128)S(1)}, u32[]{:S(2)}, u32[]{:S(2)}) async-start(s32[16,1,640]{2,1,0:T(1,128)} %broadcast_in_dim.97), calls=%async_computation | async-start | bytes 81920 | tf_op jit(solution)/shard_map/all_to_all | solution.py:99
  139.3 46.7 %collective-permute-start.2 = (bf16[256,2560]{1,0:T(8,128)(2,1)}, bf16[256,2560]{1,0:T(8,128)(2,1)}, u32[]{:S(2)}, u32[]{:S(2)}) collective-permute-start(bf16[256,2560]{1,0:T(8,128)(2,1)} %collective-permute-done.1), channel_id=1, source_target_pairs={{0,2},{2,0},{4,6},{6,4},{8,10},{10,8},{12,14},{14,12},{16,18},{18,... | collective-permute-start | bytes 3932168 | tf_op jit(solution)/shard_map/ppermute | solution.py:110
  139.5 45.3 %collective-permute-start.5 = (bf16[256,2560]{1,0:T(8,128)(2,1)}, bf16[256,2560]{1,0:T(8,128)(2,1)}, u32[]{:S(2)}, u32[]{:S(2)}) collective-permute-start(bf16[256,2560]{1,0:T(8,128)(2,1)} %collective-permute-done.3), channel_id=1, source_target_pairs={{0,4},{2,10},{4,12},{6,2},{12,20},{14,6},{20,28},{22,14},{28,24},{... | collective-permute-start | bytes 3932168 | tf_op jit(solution)/shard_map/ppermute | solution.py:109
  141.5 50.8 %collective-permute-start.4 = (bf16[256,2560]{1,0:T(8,128)(2,1)}, bf16[256,2560]{1,0:T(8,128)(2,1)S(1)}, u32[]{:S(2)}, u32[]{:S(2)}) collective-permute-start(bf16[256,2560]{1,0:T(8,128)(2,1)} %collective-permute-done.3), channel_id=1, source_target_pairs={{0,2},{2,0},{4,6},{6,4},{8,10},{10,8},{12,14},{14,12},{16,18},{18,... | collective-permute-start | bytes 3932168 | tf_op jit(solution)/shard_map/ppermute | solution.py:110
  184.8 31.4 %collective-permute-start.6 = (bf16[256,2560]{1,0:T(8,128)(2,1)}, bf16[256,2560]{1,0:T(8,128)(2,1)S(1)}, u32[]{:S(2)}, u32[]{:S(2)}) collective-permute-start(bf16[256,2560]{1,0:T(8,128)(2,1)} %collective-permute-done.5), channel_id=1, source_target_pairs={{0,2},{2,0},{4,6},{6,4},{8,10},{10,8},{12,14},{14,12},{16,18},{18,... | collective-permute-start | bytes 3932168 | tf_op jit(solution)/shard_map/ppermute | solution.py:110
  189.3 24.1 %collective-permute-start.7 = (bf16[128,2560]{1,0:T(8,128)(2,1)S(1)}, bf16[128,2560]{1,0:T(8,128)(2,1)S(1)}, u32[]{:S(2)}, u32[]{:S(2)}) collective-permute-start(bf16[128,2560]{1,0:T(8,128)(2,1)S(1)} %slice.118), channel_id=1, source_target_pairs={{0,4},{2,10},{4,12},{6,2},{12,20},{14,6},{20,28},{22,14},{28,24},{... | collective-permute-start | bytes 1966088 | tf_op jit(solution)/shard_map/ppermute | solution.py:109
  213.4 4.2 collective-permute-start.8
  218.3 24.9 %collective-permute-start.9 = (bf16[2048,256]{1,0:T(8,128)(2,1)S(1)}, bf16[2048,256]{1,0:T(8,128)(2,1)S(1)}, u32[]{:S(2)}, u32[]{:S(2)}) collective-permute-start(bf16[2048,256]{1,0:T(8,128)(2,1)S(1)} %select_convert_fusion), channel_id=1, source_target_pairs={{0,1},{1,0},{2,3},{3,2},{4,5},{5,4},{6,7},{7,6},{8,9},{9,8},{10,11... | collective-permute-start | bytes 3145736 | tf_op jit(solution)/shard_map/ppermute | solution.py:28
  253.0 53.0 %all-to-all-start.1 = ((bf16[16,256,256]{1,2,0:T(8,128)(2,1)}), bf16[16,256,256]{1,2,0:T(8,128)(2,1)S(1)}, u32[]{:S(2)}, u32[]{:S(2)}) async-start(bf16[16,256,256]{1,2,0:T(8,128)(2,1)} %copy.56), calls=%async_computation.1 | async-start | bytes 4194304 | tf_op jit(solution)/shard_map/all_to_all | solution.py:356
  259.5 194.6 %all-gather.5.cloned.1.call-start = ((), (), s32[]{:S(2)}) async-start(), calls=%async_computation.3 | async-start | bytes 13369344 | tf_op jit(solution)/shard_map/all_gather | solution.py:361
  261.6 45.8 %copy-start.22 = (f32[4,768]{1,0:T(4,128)S(1)}, f32[4,768]{1,0:T(4,128)}, u32[]{:S(2)}) copy-start(f32[4,768]{1,0:T(4,128)} %param.32) | copy-start | bytes 36868
  306.1 24.8 %collective-permute-start.10 = (bf16[8,256,256]{1,2,0:T(8,128)(2,1)S(1)}, bf16[8,256,256]{1,2,0:T(8,128)(2,1)}, u32[]{:S(2)}, u32[]{:S(2)}) collective-permute-start(bf16[8,256,256]{1,2,0:T(8,128)(2,1)S(1)} %broadcast_select_fusion.1), channel_id=1, source_target_pairs={{0,1},{1,0},{2,3},{3,2},{4,5},{5,4},{6,7},{7,6},{8,9},{9,8},{10,11... | collective-permute-start | bytes 3145736 | tf_op jit(solution)/shard_map/ppermute | solution.py:28
  338.9 2.9 collective-permute-start.11
  354.7 36.2 %copy-start.2 = (f32[512,1536]{1,0:T(8,128)}, f32[512,1536]{1,0:T(8,128)S(1)}, u32[]{:S(2)}) copy-start(f32[512,1536]{1,0:T(8,128)S(1)} %fusion.41.own_ref) | copy-start | bytes 9437188
  387.5 17.7 %collective-permute-start.12 = (bf16[512,768]{1,0:T(8,128)(2,1)}, bf16[512,768]{1,0:T(8,128)(2,1)}, u32[]{:S(2)}, u32[]{:S(2)}) collective-permute-start(bf16[512,768]{1,0:T(8,128)(2,1)} %slice.152), channel_id=1, source_target_pairs={{0,1},{1,0},{2,3},{3,2},{4,5},{5,4},{6,7},{7,6},{8,9},{9,8},{10,11... | collective-permute-start | bytes 2359304 | tf_op jit(solution)/shard_map/ppermute | solution.py:28
  388.8 33.4 %collective-permute-start.22 = (bf16[512,768]{1,0:T(8,128)(2,1)}, bf16[512,768]{1,0:T(8,128)(2,1)}, u32[]{:S(2)}, u32[]{:S(2)}) collective-permute-start(bf16[512,768]{1,0:T(8,128)(2,1)} %slice.150), channel_id=1, source_target_pairs={{0,1},{1,0},{2,3},{3,2},{4,5},{5,4},{6,7},{7,6},{8,9},{9,8},{10,11... | collective-permute-start | bytes 2359304 | tf_op jit(solution)/shard_map/ppermute | solution.py:28
  391.9 47.0 %collective-permute-start.27 = (bf16[512,768]{1,0:T(8,128)(2,1)}, bf16[512,768]{1,0:T(8,128)(2,1)S(1)}, u32[]{:S(2)}, u32[]{:S(2)}) collective-permute-start(bf16[512,768]{1,0:T(8,128)(2,1)} %slice.149), channel_id=1, source_target_pairs={{0,1},{1,0},{2,3},{3,2},{4,5},{5,4},{6,7},{7,6},{8,9},{9,8},{10,11... | collective-permute-start | bytes 2359304 | tf_op jit(solution)/shard_map/ppermute | solution.py:28
  409.4 18.2 %copy-start.14 = (bf16[512,256]{1,0:T(8,128)(2,1)S(1)}, bf16[512,256]{1,0:T(8,128)(2,1)}, u32[]{:S(2)}) copy-start(bf16[512,256]{1,0:T(8,128)(2,1)} %get-tuple-element.32) | copy-start | bytes 786436
  409.4 36.6 %collective-permute-start.13 = (bf16[512,256]{1,0:T(8,128)(2,1)}, bf16[512,256]{1,0:T(8,128)(2,1)S(1)}, u32[]{:S(2)}, u32[]{:S(2)}) collective-permute-start(bf16[512,256]{1,0:T(8,128)(2,1)} %get-tuple-element.32), channel_id=1, source_target_pairs={{0,2},{2,4},{4,6},{6,8},{8,10},{10,12},{12,14},{14,16},{16,18},{18... | collective-permute-start | bytes 786440 | tf_op jit(solution)/shard_map/ppermute | solution.py:33
  410.8 37.3 %collective-permute-start.14 = (bf16[512,256]{1,0:T(8,128)(2,1)}, bf16[512,256]{1,0:T(8,128)(2,1)S(1)}, u32[]{:S(2)}, u32[]{:S(2)}) collective-permute-start(bf16[512,256]{1,0:T(8,128)(2,1)} %get-tuple-element.32), channel_id=1, source_target_pairs={{0,4},{2,6},{4,8},{6,10},{8,12},{10,14},{12,16},{14,18},{16,20},{1... | collective-permute-start | bytes 786440 | tf_op jit(solution)/shard_map/ppermute | solution.py:33
  412.1 38.0 %collective-permute-start.15 = (bf16[512,256]{1,0:T(8,128)(2,1)}, bf16[512,256]{1,0:T(8,128)(2,1)S(1)}, u32[]{:S(2)}, u32[]{:S(2)}) collective-permute-start(bf16[512,256]{1,0:T(8,128)(2,1)} %get-tuple-element.32), channel_id=1, source_target_pairs={{0,6},{2,8},{4,10},{6,12},{8,14},{10,16},{12,18},{14,20},{16,22},{... | collective-permute-start | bytes 786440 | tf_op jit(solution)/shard_map/ppermute | solution.py:33
  422.1 30.0 %collective-permute-start.16 = (bf16[512,256]{1,0:T(8,128)(2,1)}, bf16[512,256]{1,0:T(8,128)(2,1)S(1)}, u32[]{:S(2)}, u32[]{:S(2)}) collective-permute-start(bf16[512,256]{1,0:T(8,128)(2,1)} %get-tuple-element.32), channel_id=1, source_target_pairs={{0,8},{2,10},{4,12},{6,14},{8,16},{10,18},{12,20},{14,22},{16,24},... | collective-permute-start | bytes 786440 | tf_op jit(solution)/shard_map/ppermute | solution.py:33
  438.9 26.0 %collective-permute-start.23 = (bf16[512,256]{1,0:T(8,128)(2,1)}, bf16[512,256]{1,0:T(8,128)(2,1)}, u32[]{:S(2)}, u32[]{:S(2)}) collective-permute-start(bf16[512,256]{1,0:T(8,128)(2,1)} %get-tuple-element.40), channel_id=1, source_target_pairs={{0,2},{2,4},{4,6},{6,8},{8,10},{10,12},{12,14},{14,16},{16,18},{18... | collective-permute-start | bytes 786440 | tf_op jit(solution)/shard_map/ppermute | solution.py:33
  446.0 21.4 %collective-permute-start.24 = (bf16[512,256]{1,0:T(8,128)(2,1)S(1)}, bf16[512,256]{1,0:T(8,128)(2,1)}, u32[]{:S(2)}, u32[]{:S(2)}) collective-permute-start(bf16[512,256]{1,0:T(8,128)(2,1)S(1)} %copy-done.13), channel_id=1, source_target_pairs={{0,4},{2,6},{4,8},{6,10},{8,12},{10,14},{12,16},{14,18},{16,20},{1... | collective-permute-start | bytes 786440 | tf_op jit(solution)/shard_map/ppermute | solution.py:33
  448.0 21.6 %collective-permute-start.25 = (bf16[512,256]{1,0:T(8,128)(2,1)S(1)}, bf16[512,256]{1,0:T(8,128)(2,1)}, u32[]{:S(2)}, u32[]{:S(2)}) collective-permute-start(bf16[512,256]{1,0:T(8,128)(2,1)S(1)} %copy-done.13), channel_id=1, source_target_pairs={{0,6},{2,8},{4,10},{6,12},{8,14},{10,16},{12,18},{14,20},{16,22},{... | collective-permute-start | bytes 786440 | tf_op jit(solution)/shard_map/ppermute | solution.py:33
  450.1 22.9 %collective-permute-start.26 = (bf16[512,256]{1,0:T(8,128)(2,1)S(1)}, bf16[512,256]{1,0:T(8,128)(2,1)}, u32[]{:S(2)}, u32[]{:S(2)}) collective-permute-start(bf16[512,256]{1,0:T(8,128)(2,1)S(1)} %copy-done.13), channel_id=1, source_target_pairs={{0,8},{2,10},{4,12},{6,14},{8,16},{10,18},{12,20},{14,22},{16,24},... | collective-permute-start | bytes 786440 | tf_op jit(solution)/shard_map/ppermute | solution.py:33
  452.1 23.1 %collective-permute-start.28 = (bf16[512,256]{1,0:T(8,128)(2,1)}, bf16[512,256]{1,0:T(8,128)(2,1)}, u32[]{:S(2)}, u32[]{:S(2)}) collective-permute-start(bf16[512,256]{1,0:T(8,128)(2,1)} %get-tuple-element.42), channel_id=1, source_target_pairs={{0,2},{2,4},{4,6},{6,8},{8,10},{10,12},{12,14},{14,16},{16,18},{18... | collective-permute-start | bytes 786440 | tf_op jit(solution)/shard_map/ppermute | solution.py:33
  454.1 12.3 %copy-start.18 = (bf16[5,512,256]{2,1,0:T(8,128)(2,1)S(1)}, bf16[5,512,256]{2,1,0:T(8,128)(2,1)}, u32[]{:S(2)}) copy-start(bf16[5,512,256]{2,1,0:T(8,128)(2,1)} %bitcast_dynamic-update-slice_fusion.9) | copy-start | bytes 3932164
  464.8 28.0 %copy-start.3 = (f32[512,1536]{1,0:T(8,128)}, f32[512,1536]{1,0:T(8,128)S(1)}, u32[]{:S(2)}) copy-start(f32[512,1536]{1,0:T(8,128)S(1)} %fusion.44.own_ref) | copy-start | bytes 9437188
  464.8 13.6 %collective-permute-start.29 = (bf16[512,256]{1,0:T(8,128)(2,1)S(1)}, bf16[512,256]{1,0:T(8,128)(2,1)S(1)}, u32[]{:S(2)}, u32[]{:S(2)}) collective-permute-start(bf16[512,256]{1,0:T(8,128)(2,1)S(1)} %copy-done.12), channel_id=1, source_target_pairs={{0,4},{2,6},{4,8},{6,10},{8,12},{10,14},{12,16},{14,18},{16,20},{1... | collective-permute-start | bytes 786440 | tf_op jit(solution)/shard_map/ppermute | solution.py:33
  467.4 15.2 %collective-permute-start.30 = (bf16[512,256]{1,0:T(8,128)(2,1)S(1)}, bf16[512,256]{1,0:T(8,128)(2,1)S(1)}, u32[]{:S(2)}, u32[]{:S(2)}) collective-permute-start(bf16[512,256]{1,0:T(8,128)(2,1)S(1)} %copy-done.12), channel_id=1, source_target_pairs={{0,6},{2,8},{4,10},{6,12},{8,14},{10,16},{12,18},{14,20},{16,22},{... | collective-permute-start | bytes 786440 | tf_op jit(solution)/shard_map/ppermute | solution.py:33
  469.7 23.1 %collective-permute-start.31 = (bf16[512,256]{1,0:T(8,128)(2,1)S(1)}, bf16[512,256]{1,0:T(8,128)(2,1)S(1)}, u32[]{:S(2)}, u32[]{:S(2)}) collective-permute-start(bf16[512,256]{1,0:T(8,128)(2,1)S(1)} %copy-done.12), channel_id=1, source_target_pairs={{0,8},{2,10},{4,12},{6,14},{8,16},{10,18},{12,20},{14,22},{16,24},... | collective-permute-start | bytes 786440 | tf_op jit(solution)/shard_map/ppermute | solution.py:33
  472.9 42.7 %collective-permute-start.17 = (bf16[512,768]{1,0:T(8,128)(2,1)}, bf16[512,768]{1,0:T(8,128)(2,1)}, u32[]{:S(2)}, u32[]{:S(2)}) collective-permute-start(bf16[512,768]{1,0:T(8,128)(2,1)} %slice.151), channel_id=1, source_target_pairs={{0,1},{1,0},{2,3},{3,2},{4,5},{5,4},{6,7},{7,6},{8,9},{9,8},{10,11... | collective-permute-start | bytes 2359304 | tf_op jit(solution)/shard_map/ppermute | solution.py:28
  475.1 17.6 %copy-start.19 = (bf16[5,512,256]{2,1,0:T(8,128)(2,1)}, bf16[5,512,256]{2,1,0:T(8,128)(2,1)S(1)}, u32[]{:S(2)}) copy-start(bf16[5,512,256]{2,1,0:T(8,128)(2,1)S(1)} %bitcast_dynamic-update-slice_fusion.5.kv_ref) | copy-start | bytes 3932164
  519.8 16.2 %collective-permute-start.18 = (bf16[512,256]{1,0:T(8,128)(2,1)}, bf16[512,256]{1,0:T(8,128)(2,1)S(1)}, u32[]{:S(2)}, u32[]{:S(2)}) collective-permute-start(bf16[512,256]{1,0:T(8,128)(2,1)} %get-tuple-element.36), channel_id=1, source_target_pairs={{0,2},{2,4},{4,6},{6,8},{8,10},{10,12},{12,14},{14,16},{16,18},{18... | collective-permute-start | bytes 786440 | tf_op jit(solution)/shard_map/ppermute | solution.py:33
  521.1 11.0 %copy-start.15 = (bf16[512,256]{1,0:T(8,128)(2,1)S(1)}, bf16[512,256]{1,0:T(8,128)(2,1)}, u32[]{:S(2)}) copy-start(bf16[512,256]{1,0:T(8,128)(2,1)} %get-tuple-element.36) | copy-start | bytes 786436
  532.1 20.2 %collective-permute-start.19 = (bf16[512,256]{1,0:T(8,128)(2,1)S(1)}, bf16[512,256]{1,0:T(8,128)(2,1)S(1)}, u32[]{:S(2)}, u32[]{:S(2)}) collective-permute-start(bf16[512,256]{1,0:T(8,128)(2,1)S(1)} %copy-done.15), channel_id=1, source_target_pairs={{0,4},{2,6},{4,8},{6,10},{8,12},{10,14},{12,16},{14,18},{16,20},{1... | collective-permute-start | bytes 786440 | tf_op jit(solution)/shard_map/ppermute | solution.py:33
  533.4 20.0 %collective-permute-start.20 = (bf16[512,256]{1,0:T(8,128)(2,1)S(1)}, bf16[512,256]{1,0:T(8,128)(2,1)S(1)}, u32[]{:S(2)}, u32[]{:S(2)}) collective-permute-start(bf16[512,256]{1,0:T(8,128)(2,1)S(1)} %copy-done.15), channel_id=1, source_target_pairs={{0,6},{2,8},{4,10},{6,12},{8,14},{10,16},{12,18},{14,20},{16,22},{... | collective-permute-start | bytes 786440 | tf_op jit(solution)/shard_map/ppermute | solution.py:33
  534.7 28.6 %collective-permute-start.21 = (bf16[512,256]{1,0:T(8,128)(2,1)S(1)}, bf16[512,256]{1,0:T(8,128)(2,1)S(1)}, u32[]{:S(2)}, u32[]{:S(2)}) collective-permute-start(bf16[512,256]{1,0:T(8,128)(2,1)S(1)} %copy-done.15), channel_id=1, source_target_pairs={{0,8},{2,10},{4,12},{6,14},{8,16},{10,18},{12,20},{14,22},{16,24},... | collective-permute-start | bytes 786440 | tf_op jit(solution)/shard_map/ppermute | solution.py:33
  (23 other events, 104.3 us)
Sparse Core Ops, SparseCore 0:
  13.7 238.0 all-gather.2
  306.1 98.4 all-gather.4

commit v2 on v1

--- a/solution.py
+++ b/solution.py
@@ -237,7 +237,7 @@
         )
 
 
-def attend(queries, pieces, query_segments, key_segments, need, group, groups, so_far):
+def attend(queries, pieces, column, query_segments, key_segments, need, group, groups, so_far):
     rows, width = queries.shape
     blocks, keys, _ = pieces.shape
     fixed = lambda shape: pl.BlockSpec(shape, lambda i, *_: (0,) * len(shape))
@@ -252,7 +252,7 @@
                 fixed(queries.shape),
                 fixed(query_segments.shape),
                 fixed(key_segments.shape),
-                fixed(pieces.shape),
+                pl.BlockSpec((blocks, keys, 2 * HD), lambda i, *_: (0, 0, column)),
             ]
             + [pl.BlockSpec(memory_space=pl.ANY)] * aliased,
             out_specs=pl.BlockSpec((rows, width), lambda i, *_: (0, group)),
@@ -386,47 +386,61 @@
     ends = GROUP * HD
     full = ends + 2 * HD
     output = None
-    for group in range(groups_here):
-        held_at, at = (gathered[0], group) if group < early else (gathered[1], group - early)
-
-        if group > 0:
-            if group < early:
-                held_at, product = lax.optimization_barrier((held_at, product))
-                gathered[0] = held_at
-            else:
-                hidden, pieces = lax.optimization_barrier((hidden, pieces))
-        if group > 0:
+    for held, batch in zip(gathered, (range(early), range(early, groups_here))):
+        finished = []
+        for group in batch:
+            if group == early:
+                hidden, wide = lax.optimization_barrier((hidden, wide))
+                arrivals = [wide] + [
+                    passed_along(wide, "ctx", distance) for distance in range(1, blocks)
+                ]
+                waiting = (ready, jnp.stack(arrivals))
+            elif group > 0:
+                held, product = lax.optimization_barrier((held, product))
+            columns_here = held[group - batch.start].reshape(shares * full, local_rows)
+            product = lax.dot_general(
+                hidden, columns_here, (((1,), (1,)), ((), ())), preferred_element_type=jnp.float32
+            )
+            if group == 0:
+                product, row_scale = lax.optimization_barrier((product, row_scale))
+            arrived = jnp.stack(
+                [
+                    shifted(product[:, k * full : (k + 1) * full].astype(jnp.bfloat16), "wt", k)
+                    for k in range(1, shares)
+                ]
+            )
+            finished.append(
+                finish(
+                    product,
+                    arrived,
+                    row_scale,
+                    llm_bias[group][None, :],
+                    cosine,
+                    sine,
+                    GROUP + 1,
+                    [ends, 2 * HD],
+                )
+            )
+        ready = [queries for queries, _ in finished]
+        wide = jnp.concatenate([pair for _, pair in finished], axis=1)
+    attending = [waiting] if early < groups_here else []
+    arrivals = [wide] + [passed_along(wide, "ctx", distance) for distance in range(1, blocks)]
+    attending.append((ready, jnp.stack(arrivals)))
+    group = 0
+    for ready, pieces in attending:
+        for column, queries in enumerate(ready):
             output = attend(
-                queries, pieces, query_segments, key_segments, need, group - 1, groups_here, output
-            )
-        columns_here = held_at[at].reshape(shares * full, local_rows)
-        product = lax.dot_general(
-            hidden, columns_here, (((1,), (1,)), ((), ())), preferred_element_type=jnp.float32
-        )
-        if group == 0:
-            product, row_scale = lax.optimization_barrier((product, row_scale))
-        arrived = jnp.stack(
-            [
-                shifted(product[:, k * full : (k + 1) * full].astype(jnp.bfloat16), "wt", k)
-                for k in range(1, shares)
-            ]
-        )
-        queries, pair = finish(
-            product,
-            arrived,
-            row_scale,
-            llm_bias[group][None, :],
-            cosine,
-            sine,
-            GROUP + 1,
-            [ends, 2 * HD],
-        )
-        pieces = jnp.stack(
-            [pair] + [passed_along(pair, "ctx", distance) for distance in range(1, blocks)]
-        )
-    output = attend(
-        queries, pieces, query_segments, key_segments, need, group, groups_here, output
-    )
+                queries,
+                pieces,
+                column,
+                query_segments,
+                key_segments,
+                need,
+                group,
+                groups_here,
+                output,
+            )
+            group += 1
     return output
 
 

time: 592 us -> 568 us (0.959)
  the two profiles are of different devices: /device:TPU:27 before, /device:TPU:25 now
where the time goes in v2:
time: 568 us; the launch traced here: 559 us
  waiting for transfers between devices  250 us (44%)
  Pallas kernels  79.2 us (14%)
  matrix products  71.8 us (13%)
  local copies, waits for them, and re-layouts  58.4 us (10%)
  starting transfers between devices  43.9 us (8%)
  other arithmetic  29.1 us (5%)
  between operations  25.9 us (5%)
    ppermute x4, waiting for transfers between devices, gather_features(): moving = lax.ppermute(sent, 'ctx', pairs)  104 us
    ppermute x7, waiting for transfers between devices, shifted(): lax.ppermute(value, axis, [(i, (i + steps) % count) for i in range(count)])  71.5 us
    pallas_call x4, Pallas kernels, attend(): pl.pallas_call(functools.partial(attend_kernel, aliased=aliased), out_sha...  62.7 us
    all_to_all x1, waiting for transfers between devices, on_device(): lax.all_to_all(packed.reshape(owners, slots_each, part), 'ctx', split_axi...  41.9 us
    dot_general x4, matrix products, on_device(): lax.dot_general(hidden, columns_here, (((1,), (1,)), ((), ())), preferred...  33.7 us
    unnamed x67, local copies, waits for them, and re-layouts  28 us
    all_to_all x1, waiting for transfers between devices, gather_features(): lax.all_to_all(jnp.broadcast_to(numbers[None, :], (count, numbers.shape[0...  25 us
    ppermute x8, starting transfers between devices, passed_along(): lax.ppermute(value, axis, [(i, i + steps) for i in range(count - steps)])  17.7 us
  transfers between devices with their start and end apart: 28, of which 13 were waited for; matrix products, arithmetic and copies ran while one was open for 23% of the time, Pallas kernels for 11%

profile of v2, /device:TPU:25, one launch (start us, length us, event | category | flops | bytes accessed | tf_op | source)
XLA Modules:
  0.0 558.6 jit_solution(11040138110505045529)
XLA Ops:
  7.2 2.9 fusion.12
  13.6 8.3 %copy.50 = bf16[1280,3,640]{0,2,1:T(8,128)(2,1)} copy(bf16[1280,3,640]{2,0,1:T(8,128)(2,1)} %param.20) | data formatting | bytes 9830400 | tf_op args[2]
  23.0 5.7 %add_convert_fusion.1 = bf16[512,3,640]{2,0,1:T(8,128)(2,1)S(1)} fusion(f32[3,640]{1,0:T(4,128)S(1)} %copy-done.25, bf16[1280,3,640]{0,2,1:T(8,128)(2,1)} %copy.50, f32[]{:T(128)S(6)} %convert.21, bf16[512,1280]{1,0:T(8,128)(2,1)S(1)} %copy-done.9, f32[1280]{0:T(1024)S(1)} %copy-done.26, f32[512]{0:T(512)S(1)} %add_rsqrt_fusion.1), kind=kOutput, calls=%fused_computation.23 | convolution fusion | flops 2528542720 | bytes 8206852 | tf_op jit(solution)/shard_map/dot_general | solution.py:51
  29.9 5.5 fusion.40
  35.4 4.6 fusion.23
  40.8 2.1 reshape_reshape.3
  43.5 2.4 collective-permute-done
  47.6 44.5 %collective-permute-done.1 = bf16[256,2560]{1,0:T(8,128)(2,1)} collective-permute-done((bf16[256,2560]{1,0:T(8,128)(2,1)S(1)}, bf16[256,2560]{1,0:T(8,128)(2,1)}, u32[]{:S(2)}, u32[]{:S(2)}) %collective-permute-start.1) | collective-permute-done | bytes 1310752 | tf_op jit(solution)/shard_map/ppermute | solution.py:109
  93.3 6.9 %all-to-all-start = ((s32[16,1,640]{2,1,0:T(1,128)}), s32[16,1,640]{2,1,0:T(1,128)S(1)}, u32[]{:S(2)}, u32[]{:S(2)}) async-start(s32[16,1,640]{2,1,0:T(1,128)} %broadcast_in_dim.97), calls=%async_computation | async-start | bytes 81920 | tf_op jit(solution)/shard_map/all_to_all | solution.py:99
  112.7 2.3 multiply_convert_fusion.2
  115.1 25.0 %all-to-all-done = s32[16,1,640]{2,1,0:T(1,128)S(1)} async-done(((s32[16,1,640]{2,1,0:T(1,128)}), s32[16,1,640]{2,1,0:T(1,128)S(1)}, u32[]{:S(2)}, u32[]{:S(2)}) %all-to-all-start) | async-done | bytes 40992 | tf_op jit(solution)/shard_map/all_to_all | solution.py:99
  142.9 2.2 convolution_dynamic-update-slice_fusion.6
  145.1 2.1 convolution_dynamic-update-slice_fusion.5
  147.2 38.4 %collective-permute-done.5 = bf16[256,2560]{1,0:T(8,128)(2,1)} collective-permute-done((bf16[256,2560]{1,0:T(8,128)(2,1)}, bf16[256,2560]{1,0:T(8,128)(2,1)}, u32[]{:S(2)}, u32[]{:S(2)}) %collective-permute-start.5) | collective-permute-done | bytes 1310752 | tf_op jit(solution)/shard_map/ppermute | solution.py:109
  186.7 2.2 convolution_dynamic-update-slice_fusion.4
  190.5 2.1 convolution_dynamic-update-slice_fusion.3
  193.5 20.6 %collective-permute-done.7 = bf16[128,2560]{1,0:T(8,128)(2,1)S(1)} collective-permute-done((bf16[128,2560]{1,0:T(8,128)(2,1)S(1)}, bf16[128,2560]{1,0:T(8,128)(2,1)S(1)}, u32[]{:S(2)}, u32[]{:S(2)}) %collective-permute-start.7) | collective-permute-done | bytes 655392 | tf_op jit(solution)/shard_map/ppermute | solution.py:109
  214.8 2.1 convolution_dynamic-update-slice_fusion.1
  220.3 9.0 %fusion.1 = bf16[4096,2048]{1,0:T(8,128)(2,1)S(1)} fusion(s32[2048]{0:T(1024)S(1)} %select_bitcast_fusion.2), kind=kLoop, calls=%fused_computation.4 | loop fusion | flops 16777216 | bytes 16785408 | tf_op jit(solution)/shard_map/convert_element_type | solution.py:353
  229.9 14.0 %collective-permute-done.9 = bf16[2048,256]{1,0:T(8,128)(2,1)S(1)} collective-permute-done((bf16[2048,256]{1,0:T(8,128)(2,1)S(1)}, bf16[2048,256]{1,0:T(8,128)(2,1)S(1)}, u32[]{:S(2)}, u32[]{:S(2)}) %collective-permute-start.9) | collective-permute-done | bytes 1048608 | tf_op jit(solution)/shard_map/ppermute | solution.py:28
  243.9 7.5 %convolution_convert_fusion = bf16[4096,256]{1,0:T(8,128)(2,1)S(1)} fusion(bf16[4096,2048]{1,0:T(8,128)(2,1)S(1)} %fusion.1, bf16[2048,256]{1,0:T(8,128)(2,1)S(1)} %collective-permute-done.9, f32[2048,512]{1,0:T(8,128)} %copy-done.10, pred[]{:T(512)S(6)} %select_n.243), kind=kOutput, calls=%fused_computation.14 | convolution fusion | flops 4298113024 | bytes 24117248 | tf_op jit(solution)/shard_map/dot_general | solution.py:355
  251.4 2.4 copy.56
  253.8 5.7 %all-to-all-start.1 = ((bf16[16,256,256]{1,2,0:T(8,128)(2,1)}), bf16[16,256,256]{1,2,0:T(8,128)(2,1)S(1)}, u32[]{:S(2)}, u32[]{:S(2)}) async-start(bf16[16,256,256]{1,2,0:T(8,128)(2,1)} %copy.56), calls=%async_computation.1 | async-start | bytes 4194304 | tf_op jit(solution)/shard_map/all_to_all | solution.py:356
  261.8 41.9 %all-to-all-done.1 = bf16[16,256,256]{1,2,0:T(8,128)(2,1)S(1)} async-done(((bf16[16,256,256]{1,2,0:T(8,128)(2,1)}), bf16[16,256,256]{1,2,0:T(8,128)(2,1)S(1)}, u32[]{:S(2)}, u32[]{:S(2)}) %all-to-all-start.1) | async-done | bytes 2097184 | tf_op jit(solution)/shard_map/all_to_all | solution.py:356
  305.2 24.0 %collective-permute-done.10 = bf16[8,256,256]{1,2,0:T(8,128)(2,1)} collective-permute-done((bf16[8,256,256]{1,2,0:T(8,128)(2,1)S(1)}, bf16[8,256,256]{1,2,0:T(8,128)(2,1)}, u32[]{:S(2)}, u32[]{:S(2)}) %collective-permute-start.10) | collective-permute-done | bytes 1048608 | tf_op jit(solution)/shard_map/ppermute | solution.py:28
  334.2 2.1 copy-done.6
  340.1 4.7 slice-done
  346.3 6.7 %fusion.41.own_ref = f32[512,1536]{1,0:T(8,128)S(1)} fusion(bf16[512,4096]{1,0:T(8,128)(2,1)S(1)} %copy-done.7, bf16[1536,4096]{1,0:T(8,128)(2,1)S(1)} %bitcast.155), kind=kOutput, calls=%fused_computation.127 | convolution fusion | flops 6442450944 | bytes 19922944 | tf_op jit(solution)/shard_map/dot_general | solution.py:401
  354.9 4.1 slice-done.1
  359.0 9.5 %fusion.42.own_ref = f32[512,1536]{1,0:T(8,128)S(1)} fusion(bf16[512,4096]{1,0:T(8,128)(2,1)} %copy-done.6, bf16[1536,4096]{1,0:T(8,128)(2,1)S(1)} %bitcast.156), kind=kOutput, calls=%fused_computation.128 | convolution fusion | flops 6442450944 | bytes 19922944 | tf_op jit(solution)/shard_map/dot_general | solution.py:401
  371.0 3.4 slice-done.2
  375.6 6.7 %fusion.43.own_ref = f32[512,1536]{1,0:T(8,128)S(1)} fusion(bf16[512,4096]{1,0:T(8,128)(2,1)S(1)} %copy-done.8, bf16[1536,4096]{1,0:T(8,128)(2,1)S(1)} %bitcast.157), kind=kOutput, calls=%fused_computation.129 | convolution fusion | flops 6442450944 | bytes 19922944 | tf_op jit(solution)/shard_map/dot_general | solution.py:401
  388.7 4.1 finish.4
  392.9 11.8 %collective-permute-done.13 = bf16[512,768]{1,0:T(8,128)(2,1)} collective-permute-done((bf16[512,768]{1,0:T(8,128)(2,1)}, bf16[512,768]{1,0:T(8,128)(2,1)}, u32[]{:S(2)}, u32[]{:S(2)}) %collective-permute-start.13) | collective-permute-done | bytes 786464 | tf_op jit(solution)/shard_map/ppermute | solution.py:28
  404.6 4.1 finish.5
  408.7 12.8 %collective-permute-done.14 = bf16[512,768]{1,0:T(8,128)(2,1)} collective-permute-done((bf16[512,768]{1,0:T(8,128)(2,1)}, bf16[512,768]{1,0:T(8,128)(2,1)}, u32[]{:S(2)}, u32[]{:S(2)}) %collective-permute-start.14) | collective-permute-done | bytes 786464 | tf_op jit(solution)/shard_map/ppermute | solution.py:28
  421.5 4.1 finish.6
  426.6 6.7 %collective-permute-start.20 = (bf16[512,768]{1,0:T(8,128)(2,1)S(1)}, bf16[512,768]{1,0:T(8,128)(2,1)}, u32[]{:S(2)}, u32[]{:S(2)}) collective-permute-start(bf16[512,768]{1,0:T(8,128)(2,1)S(1)} %pad_maximum_fusion.3), channel_id=1, source_target_pairs={{0,2},{2,4},{4,6},{6,8},{8,10},{10,12},{12,14},{14,16},{16,18},{18... | collective-permute-start | bytes 2359304 | tf_op jit(solution)/shard_map/ppermute | solution.py:33
  433.4 10.8 %fusion.44.own_ref = f32[512,1536]{1,0:T(8,128)S(1)} fusion(bf16[512,4096]{1,0:T(8,128)(2,1)} %copy-done.6, bf16[1536,4096]{1,0:T(8,128)(2,1)} %bitcast.185), kind=kOutput, calls=%fused_computation.130 | convolution fusion | flops 6442450944 | bytes 19922944 | tf_op jit(solution)/shard_map/dot_general | solution.py:401
  454.9 7.9 %collective-permute-done.15 = bf16[512,768]{1,0:T(8,128)(2,1)S(1)} collective-permute-done((bf16[512,768]{1,0:T(8,128)(2,1)}, bf16[512,768]{1,0:T(8,128)(2,1)S(1)}, u32[]{:S(2)}, u32[]{:S(2)}) %collective-permute-start.15) | collective-permute-done | bytes 786464 | tf_op jit(solution)/shard_map/ppermute | solution.py:28
  463.7 4.1 finish.7
  471.8 2.1 bitcast_dynamic-update-slice_fusion.3
  475.2 2.1 bitcast_dynamic-update-slice_fusion.2
  477.2 6.0 %collective-permute-done.22 = bf16[512,768]{1,0:T(8,128)(2,1)} collective-permute-done((bf16[512,768]{1,0:T(8,128)(2,1)S(1)}, bf16[512,768]{1,0:T(8,128)(2,1)}, u32[]{:S(2)}, u32[]{:S(2)}) %collective-permute-start.22) | collective-permute-done | bytes 786464 | tf_op jit(solution)/shard_map/ppermute | solution.py:33
  487.5 15.7 %attend.4.refs_0_ = bf16[512,2048]{1,0:T(8,128)(2,1)} custom-call(s32[5]{0:T(128)} %and_convert_fusion.need, bf16[512,512]{1,0:T(8,128)(2,1)} %get-tuple-element.42.q_ref, s32[1,512]{1,0:T(1,128)} %bitcast.178, s32[5,512,1]{2,1,0:T(8,128)} %broadcast_select_fusion.4.kseg_ref, bf16[5,512,768]{2,1,0:T(8,128)(2,1)} %bitcast_dynamic-update-slice_fusion.kv_ref), custom_call_target="tpu_custom_call" | custom-call | flops 2684354560 | bytes 2097152 | tf_op jit(solution)/shard_map/attend/pallas_call | solution.py:245
  503.2 15.7 %attend.5.refs_0_ = bf16[512,2048]{1,0:T(8,128)(2,1)} custom-call(s32[5]{0:T(128)} %and_convert_fusion.need, bf16[512,512]{1,0:T(8,128)(2,1)} %get-tuple-element.41.q_ref, s32[1,512]{1,0:T(1,128)} %bitcast.179, s32[5,512,1]{2,1,0:T(8,128)} %broadcast_select_fusion.4.kseg_ref, ...), custom_call_target="tpu_custom_call", output_to_operand_aliasing={{}: (5, {})} | custom-call | flops 2684354560 | bytes 2097152 | tf_op jit(solution)/shard_map/attend/pallas_call | solution.py:245
  518.9 15.7 %attend.6.refs_0_ = bf16[512,2048]{1,0:T(8,128)(2,1)} custom-call(s32[5]{0:T(128)} %and_convert_fusion.need, bf16[512,512]{1,0:T(8,128)(2,1)} %get-tuple-element.39.q_ref, s32[1,512]{1,0:T(1,128)} %bitcast.180, s32[5,512,1]{2,1,0:T(8,128)} %broadcast_select_fusion.4.kseg_ref, ...), custom_call_target="tpu_custom_call", output_to_operand_aliasing={{}: (5, {})} | custom-call | flops 2684354560 | bytes 2097152 | tf_op jit(solution)/shard_map/attend/pallas_call | solution.py:245
  535.8 15.7 %attend.7 = bf16[512,2048]{1,0:T(8,128)(2,1)} custom-call(s32[5]{0:T(128)} %and_convert_fusion.need, bf16[512,512]{1,0:T(8,128)(2,1)} %get-tuple-element.37.q_ref, s32[1,512]{1,0:T(1,128)} %bitcast.181, s32[5,512,1]{2,1,0:T(8,128)} %broadcast_select_fusion.4.kseg_ref, bf16[5,512,256]{2,1,0:T(8,128)(2,1)} %copy-done.16, ...), custom_call_target="tpu_custom_call", output_to_operand_aliasing={{}: (5, {})} | custom-call | flops 2684354560 | bytes 2097152 | tf_op jit(solution)/shard_map/attend/pallas_call | solution.py:245
  (181 shorter events, 71.9 us)
Async XLA Ops:
  6.5 333.6 %all-gather.3.cloned.1.call-start = ((), (), s32[]{:S(2)}) async-start(), calls=%async_computation.2 | async-start | bytes 40108032 | tf_op jit(solution)/shard_map/all_gather | solution.py:326
  13.6 9.0 %copy-start.9 = (bf16[512,1280]{1,0:T(8,128)(2,1)S(1)}, bf16[512,1280]{1,0:T(8,128)(2,1)}, u32[]{:S(2)}) copy-start(bf16[512,1280]{1,0:T(8,128)(2,1)} %param.18) | copy-start | bytes 3932164
  13.6 9.3 %copy-start.25 = (f32[3,640]{1,0:T(4,128)S(1)}, f32[3,640]{1,0:T(4,128)}, u32[]{:S(2)}) copy-start(f32[3,640]{1,0:T(4,128)} %param.22) | copy-start | bytes 23044
  13.6 9.3 %copy-start.26 = (f32[1280]{0:T(1024)S(1)}, f32[1280]{0:T(1024)}, u32[]{:S(2)}) copy-start(f32[1280]{0:T(1024)} %param.19) | copy-start | bytes 15364
  40.0 52.7 %copy-start.18 = (s32[512]{0:T(512)S(1)}, s32[512]{0:T(512)}, u32[]{:S(2)}) copy-start(s32[512]{0:T(512)} %param.33) | copy-start | bytes 6148
  40.0 52.7 %copy-start.22 = (s32[128]{0:T(128)S(1)}, s32[128]{0:T(128)}, u32[]{:S(2)}) copy-start(s32[128]{0:T(128)} %param.27) | copy-start | bytes 1540
  40.7 59.5 %copy-start.27 = (s32[8]{0:T(128)S(1)}, s32[8]{0:T(128)}, u32[]{:S(2)}) copy-start(s32[8]{0:T(128)} %constant.193.clone) | copy-start | bytes 100
  40.8 65.7 %copy-start.17 = (s32[8]{0:T(128)S(1)}, s32[8]{0:T(128)}, u32[]{:S(2)}) copy-start(s32[8]{0:T(128)} %constant.192.clone) | copy-start | bytes 100
  40.8 70.3 %copy-start.21 = (bf16[1,1,512]{2,1,0:T(2,128)(2,1)S(1)}, bf16[1,1,512]{2,1,0:T(2,128)(2,1)}, u32[]{:S(2)}) copy-start(bf16[1,1,512]{2,1,0:T(2,128)(2,1)} %param.25) | copy-start | bytes 3076
  42.9 3.0 collective-permute-start
  47.0 45.1 %collective-permute-start.1 = (bf16[256,2560]{1,0:T(8,128)(2,1)S(1)}, bf16[256,2560]{1,0:T(8,128)(2,1)}, u32[]{:S(2)}, u32[]{:S(2)}) collective-permute-start(bf16[256,2560]{1,0:T(8,128)(2,1)S(1)} %constant_dynamic-update-slice_fusion), channel_id=1, source_target_pairs={{0,4},{2,10},{4,12},{6,2},{12,20},{14,6},{20,28},{22,14},{28,24},{... | collective-permute-start | bytes 3932168 | tf_op jit(solution)/shard_map/ppermute | solution.py:109
  92.1 48.3 %collective-permute-start.3 = (bf16[256,2560]{1,0:T(8,128)(2,1)}, bf16[256,2560]{1,0:T(8,128)(2,1)}, u32[]{:S(2)}, u32[]{:S(2)}) collective-permute-start(bf16[256,2560]{1,0:T(8,128)(2,1)} %collective-permute-done.1), channel_id=1, source_target_pairs={{0,4},{2,10},{4,12},{6,2},{12,20},{14,6},{20,28},{22,14},{28,24},{... | collective-permute-start | bytes 3932168 | tf_op jit(solution)/shard_map/ppermute | solution.py:109
  93.3 46.7 %all-to-all-start = ((s32[16,1,640]{2,1,0:T(1,128)}), s32[16,1,640]{2,1,0:T(1,128)S(1)}, u32[]{:S(2)}, u32[]{:S(2)}) async-start(s32[16,1,640]{2,1,0:T(1,128)} %broadcast_in_dim.97), calls=%async_computation | async-start | bytes 81920 | tf_op jit(solution)/shard_map/all_to_all | solution.py:99
  140.0 46.7 %collective-permute-start.2 = (bf16[256,2560]{1,0:T(8,128)(2,1)}, bf16[256,2560]{1,0:T(8,128)(2,1)}, u32[]{:S(2)}, u32[]{:S(2)}) collective-permute-start(bf16[256,2560]{1,0:T(8,128)(2,1)} %collective-permute-done.1), channel_id=1, source_target_pairs={{0,2},{2,0},{4,6},{6,4},{8,10},{10,8},{12,14},{14,12},{16,18},{18,... | collective-permute-start | bytes 3932168 | tf_op jit(solution)/shard_map/ppermute | solution.py:110
  140.4 45.3 %collective-permute-start.5 = (bf16[256,2560]{1,0:T(8,128)(2,1)}, bf16[256,2560]{1,0:T(8,128)(2,1)}, u32[]{:S(2)}, u32[]{:S(2)}) collective-permute-start(bf16[256,2560]{1,0:T(8,128)(2,1)} %collective-permute-done.3), channel_id=1, source_target_pairs={{0,4},{2,10},{4,12},{6,2},{12,20},{14,6},{20,28},{22,14},{28,24},{... | collective-permute-start | bytes 3932168 | tf_op jit(solution)/shard_map/ppermute | solution.py:109
  142.0 50.6 %collective-permute-start.4 = (bf16[256,2560]{1,0:T(8,128)(2,1)}, bf16[256,2560]{1,0:T(8,128)(2,1)S(1)}, u32[]{:S(2)}, u32[]{:S(2)}) collective-permute-start(bf16[256,2560]{1,0:T(8,128)(2,1)} %collective-permute-done.3), channel_id=1, source_target_pairs={{0,2},{2,0},{4,6},{6,4},{8,10},{10,8},{12,14},{14,12},{16,18},{18,... | collective-permute-start | bytes 3932168 | tf_op jit(solution)/shard_map/ppermute | solution.py:110
  185.7 31.3 %collective-permute-start.6 = (bf16[256,2560]{1,0:T(8,128)(2,1)}, bf16[256,2560]{1,0:T(8,128)(2,1)S(1)}, u32[]{:S(2)}, u32[]{:S(2)}) collective-permute-start(bf16[256,2560]{1,0:T(8,128)(2,1)} %collective-permute-done.5), channel_id=1, source_target_pairs={{0,2},{2,0},{4,6},{6,4},{8,10},{10,8},{12,14},{14,12},{16,18},{18,... | collective-permute-start | bytes 3932168 | tf_op jit(solution)/shard_map/ppermute | solution.py:110
  190.0 24.1 %collective-permute-start.7 = (bf16[128,2560]{1,0:T(8,128)(2,1)S(1)}, bf16[128,2560]{1,0:T(8,128)(2,1)S(1)}, u32[]{:S(2)}, u32[]{:S(2)}) collective-permute-start(bf16[128,2560]{1,0:T(8,128)(2,1)S(1)} %slice.118), channel_id=1, source_target_pairs={{0,4},{2,10},{4,12},{6,2},{12,20},{14,6},{20,28},{22,14},{28,24},{... | collective-permute-start | bytes 1966088 | tf_op jit(solution)/shard_map/ppermute | solution.py:109
  214.1 4.2 collective-permute-start.8
  218.8 10.5 %copy-start.10 = (f32[2048,512]{1,0:T(8,128)}, f32[2048,512]{1,0:T(8,128)S(1)}, u32[]{:S(2)}) copy-start(f32[2048,512]{1,0:T(8,128)S(1)} %convolution_dynamic-update-slice_fusion.7) | copy-start | bytes 12582916
  219.1 24.9 %collective-permute-start.9 = (bf16[2048,256]{1,0:T(8,128)(2,1)S(1)}, bf16[2048,256]{1,0:T(8,128)(2,1)S(1)}, u32[]{:S(2)}, u32[]{:S(2)}) collective-permute-start(bf16[2048,256]{1,0:T(8,128)(2,1)S(1)} %select_convert_fusion), channel_id=1, source_target_pairs={{0,1},{1,0},{2,3},{3,2},{4,5},{5,4},{6,7},{7,6},{8,9},{9,8},{10,11... | collective-permute-start | bytes 3145736 | tf_op jit(solution)/shard_map/ppermute | solution.py:28
  253.8 50.0 %all-to-all-start.1 = ((bf16[16,256,256]{1,2,0:T(8,128)(2,1)}), bf16[16,256,256]{1,2,0:T(8,128)(2,1)S(1)}, u32[]{:S(2)}, u32[]{:S(2)}) async-start(bf16[16,256,256]{1,2,0:T(8,128)(2,1)} %copy.56), calls=%async_computation.1 | async-start | bytes 4194304 | tf_op jit(solution)/shard_map/all_to_all | solution.py:356
  259.5 173.9 %all-gather.5.cloned.1.call-start = ((), (), s32[]{:S(2)}) async-start(), calls=%async_computation.3 | async-start | bytes 13369344 | tf_op jit(solution)/shard_map/all_gather | solution.py:361
  303.8 25.3 %collective-permute-start.10 = (bf16[8,256,256]{1,2,0:T(8,128)(2,1)S(1)}, bf16[8,256,256]{1,2,0:T(8,128)(2,1)}, u32[]{:S(2)}, u32[]{:S(2)}) collective-permute-start(bf16[8,256,256]{1,2,0:T(8,128)(2,1)S(1)} %broadcast_select_fusion.1), channel_id=1, source_target_pairs={{0,1},{1,0},{2,3},{3,2},{4,5},{5,4},{6,7},{7,6},{8,9},{9,8},{10,11... | collective-permute-start | bytes 3145736 | tf_op jit(solution)/shard_map/ppermute | solution.py:28
  337.2 2.9 collective-permute-start.11
  340.1 4.7 slice-start
  340.1 6.1 %copy-start.7 = (bf16[512,4096]{1,0:T(8,128)(2,1)S(1)}, bf16[512,4096]{1,0:T(8,128)(2,1)}, u32[]{:S(2)}) copy-start(bf16[512,4096]{1,0:T(8,128)(2,1)} %copy-done.6) | copy-start | bytes 12582916
  354.0 4.9 slice-start.1
  369.6 4.9 slice-start.2
  369.6 6.1 %copy-start.8 = (bf16[512,4096]{1,0:T(8,128)(2,1)S(1)}, bf16[512,4096]{1,0:T(8,128)(2,1)}, u32[]{:S(2)}) copy-start(bf16[512,4096]{1,0:T(8,128)(2,1)} %copy-done.6) | copy-start | bytes 12582916
  369.6 19.1 %collective-permute-start.12 = (bf16[512,768]{1,0:T(8,128)(2,1)}, bf16[512,768]{1,0:T(8,128)(2,1)}, u32[]{:S(2)}, u32[]{:S(2)}) collective-permute-start(bf16[512,768]{1,0:T(8,128)(2,1)} %slice.152), channel_id=1, source_target_pairs={{0,1},{1,0},{2,3},{3,2},{4,5},{5,4},{6,7},{7,6},{8,9},{9,8},{10,11... | collective-permute-start | bytes 2359304 | tf_op jit(solution)/shard_map/ppermute | solution.py:28
  370.8 33.8 %collective-permute-start.13 = (bf16[512,768]{1,0:T(8,128)(2,1)}, bf16[512,768]{1,0:T(8,128)(2,1)}, u32[]{:S(2)}, u32[]{:S(2)}) collective-permute-start(bf16[512,768]{1,0:T(8,128)(2,1)} %slice.151), channel_id=1, source_target_pairs={{0,1},{1,0},{2,3},{3,2},{4,5},{5,4},{6,7},{7,6},{8,9},{9,8},{10,11... | collective-permute-start | bytes 2359304 | tf_op jit(solution)/shard_map/ppermute | solution.py:28
  375.6 9.1 %copy-start.19 = (f32[4,768]{1,0:T(4,128)S(1)}, f32[4,768]{1,0:T(4,128)}, u32[]{:S(2)}) copy-start(f32[4,768]{1,0:T(4,128)} %param.32) | copy-start | bytes 36868
  382.4 10.5 %copy-start.3 = (f32[512,1536]{1,0:T(8,128)}, f32[512,1536]{1,0:T(8,128)S(1)}, u32[]{:S(2)}) copy-start(f32[512,1536]{1,0:T(8,128)S(1)} %fusion.43.own_ref) | copy-start | bytes 9437188
  383.4 38.0 %collective-permute-start.14 = (bf16[512,768]{1,0:T(8,128)(2,1)}, bf16[512,768]{1,0:T(8,128)(2,1)}, u32[]{:S(2)}, u32[]{:S(2)}) collective-permute-start(bf16[512,768]{1,0:T(8,128)(2,1)} %slice.150), channel_id=1, source_target_pairs={{0,1},{1,0},{2,3},{3,2},{4,5},{5,4},{6,7},{7,6},{8,9},{9,8},{10,11... | collective-permute-start | bytes 2359304 | tf_op jit(solution)/shard_map/ppermute | solution.py:28
  408.7 16.9 %copy-start.14 = (bf16[512,256]{1,0:T(8,128)(2,1)S(1)}, bf16[512,256]{1,0:T(8,128)(2,1)}, u32[]{:S(2)}) copy-start(bf16[512,256]{1,0:T(8,128)(2,1)} %get-tuple-element.30) | copy-start | bytes 786436
  408.7 16.9 %copy-start.15 = (bf16[512,256]{1,0:T(8,128)(2,1)S(1)}, bf16[512,256]{1,0:T(8,128)(2,1)}, u32[]{:S(2)}) copy-start(bf16[512,256]{1,0:T(8,128)(2,1)} %get-tuple-element.32) | copy-start | bytes 786436
  426.6 43.3 %collective-permute-start.20 = (bf16[512,768]{1,0:T(8,128)(2,1)S(1)}, bf16[512,768]{1,0:T(8,128)(2,1)}, u32[]{:S(2)}, u32[]{:S(2)}) collective-permute-start(bf16[512,768]{1,0:T(8,128)(2,1)S(1)} %pad_maximum_fusion.3), channel_id=1, source_target_pairs={{0,2},{2,4},{4,6},{6,8},{8,10},{10,12},{12,14},{14,16},{16,18},{18... | collective-permute-start | bytes 2359304 | tf_op jit(solution)/shard_map/ppermute | solution.py:33
  444.1 3.1 copy-start.5
  445.2 17.6 %collective-permute-start.15 = (bf16[512,768]{1,0:T(8,128)(2,1)}, bf16[512,768]{1,0:T(8,128)(2,1)S(1)}, u32[]{:S(2)}, u32[]{:S(2)}) collective-permute-start(bf16[512,768]{1,0:T(8,128)(2,1)} %slice.149), channel_id=1, source_target_pairs={{0,1},{1,0},{2,3},{3,2},{4,5},{5,4},{6,7},{7,6},{8,9},{9,8},{10,11... | collective-permute-start | bytes 2359304 | tf_op jit(solution)/shard_map/ppermute | solution.py:28
  448.2 25.7 %collective-permute-start.21 = (bf16[512,768]{1,0:T(8,128)(2,1)S(1)}, bf16[512,768]{1,0:T(8,128)(2,1)}, u32[]{:S(2)}, u32[]{:S(2)}) collective-permute-start(bf16[512,768]{1,0:T(8,128)(2,1)S(1)} %pad_maximum_fusion.3), channel_id=1, source_target_pairs={{0,4},{2,6},{4,8},{6,10},{8,12},{10,14},{12,16},{14,18},{16,20},{1... | collective-permute-start | bytes 2359304 | tf_op jit(solution)/shard_map/ppermute | solution.py:33
  451.4 31.8 %collective-permute-start.22 = (bf16[512,768]{1,0:T(8,128)(2,1)S(1)}, bf16[512,768]{1,0:T(8,128)(2,1)}, u32[]{:S(2)}, u32[]{:S(2)}) collective-permute-start(bf16[512,768]{1,0:T(8,128)(2,1)S(1)} %pad_maximum_fusion.3), channel_id=1, source_target_pairs={{0,6},{2,8},{4,10},{6,12},{8,14},{10,16},{12,18},{14,20},{16,22},{... | collective-permute-start | bytes 2359304 | tf_op jit(solution)/shard_map/ppermute | solution.py:33
  452.7 33.9 %collective-permute-start.23 = (bf16[512,768]{1,0:T(8,128)(2,1)S(1)}, bf16[512,768]{1,0:T(8,128)(2,1)S(1)}, u32[]{:S(2)}, u32[]{:S(2)}) collective-permute-start(bf16[512,768]{1,0:T(8,128)(2,1)S(1)} %pad_maximum_fusion.3), channel_id=1, source_target_pairs={{0,8},{2,10},{4,12},{6,14},{8,16},{10,18},{12,20},{14,22},{16,24},... | collective-permute-start | bytes 2359304 | tf_op jit(solution)/shard_map/ppermute | solution.py:33
  467.8 15.4 %copy-start.13 = (bf16[512,256]{1,0:T(8,128)(2,1)S(1)}, bf16[512,256]{1,0:T(8,128)(2,1)}, u32[]{:S(2)}) copy-start(bf16[512,256]{1,0:T(8,128)(2,1)} %get-tuple-element.38) | copy-start | bytes 786436
  467.8 66.8 %collective-permute-start.16 = (bf16[512,256]{1,0:T(8,128)(2,1)}, bf16[512,256]{1,0:T(8,128)(2,1)S(1)}, u32[]{:S(2)}, u32[]{:S(2)}) collective-permute-start(bf16[512,256]{1,0:T(8,128)(2,1)} %get-tuple-element.38), channel_id=1, source_target_pairs={{0,2},{2,4},{4,6},{6,8},{8,10},{10,12},{12,14},{14,16},{16,18},{18... | collective-permute-start | bytes 786440 | tf_op jit(solution)/shard_map/ppermute | solution.py:33
  469.9 64.7 %collective-permute-start.17 = (bf16[512,256]{1,0:T(8,128)(2,1)}, bf16[512,256]{1,0:T(8,128)(2,1)S(1)}, u32[]{:S(2)}, u32[]{:S(2)}) collective-permute-start(bf16[512,256]{1,0:T(8,128)(2,1)} %get-tuple-element.38), channel_id=1, source_target_pairs={{0,4},{2,6},{4,8},{6,10},{8,12},{10,14},{12,16},{14,18},{16,20},{1... | collective-permute-start | bytes 786440 | tf_op jit(solution)/shard_map/ppermute | solution.py:33
  473.9 60.8 %collective-permute-start.18 = (bf16[512,256]{1,0:T(8,128)(2,1)}, bf16[512,256]{1,0:T(8,128)(2,1)S(1)}, u32[]{:S(2)}, u32[]{:S(2)}) collective-permute-start(bf16[512,256]{1,0:T(8,128)(2,1)} %get-tuple-element.38), channel_id=1, source_target_pairs={{0,6},{2,8},{4,10},{6,12},{8,14},{10,16},{12,18},{14,20},{16,22},{... | collective-permute-start | bytes 786440 | tf_op jit(solution)/shard_map/ppermute | solution.py:33
  483.2 51.5 %collective-permute-start.19 = (bf16[512,256]{1,0:T(8,128)(2,1)S(1)}, bf16[512,256]{1,0:T(8,128)(2,1)S(1)}, u32[]{:S(2)}, u32[]{:S(2)}) collective-permute-start(bf16[512,256]{1,0:T(8,128)(2,1)S(1)} %copy-done.13), channel_id=1, source_target_pairs={{0,8},{2,10},{4,12},{6,14},{8,16},{10,18},{12,20},{14,22},{16,24},... | collective-permute-start | bytes 786440 | tf_op jit(solution)/shard_map/ppermute | solution.py:33
  (11 other events, 17.0 us)
Sparse Core Ops, SparseCore 0:
  13.7 238.7 all-gather.2
  303.9 101.7 all-gather.4
